TPU v7x, 768 devices: a whole 4x8x12 slice. The times are simulated.
768 devices in a mesh: rep: 96 (over x, z, core), shard: 8 (over y).
Axes of the slice: x: 4, y: 8, z: 12, core: 2. Of those that a mesh axis runs over, the one named last changes fastest.
Arguments:
- inputs: bfloat16 [36864, 2048], P('rep', 'shard'), may hold values from -6 to 6
- cotangent: bfloat16 [36864, 6144], P('rep'), may hold values from -0.109375 to 0.109375
- momentum: float32 [6144, 2048], P('rep', 'shard'), may hold values from -54 to 54
- right_prev: float32 [2048, 64], P('shard'), may hold values from -0.125 to 0.125
Outputs:
- new_momentum: float32 [6144, 2048], P('rep', 'shard')
- right_factor: float32 [2048, 64], P('shard')
- update: bfloat16 [6144, 2048], P('rep', 'shard')
All inputs are finite; a program needn't handle non-finite values.
Results may differ from a plain program's by a relative error of at most 0.001.
Values sent between devices are 32-bit elements; how exact they have to be, the bound alone decides.
No kernel may reach another device: no remote copies, remote signals or barrier semaphores. Data moves between devices by JAX's collectives and lax.ppermute only.
A program may use at most 64 MiB of HBM per device.

v0:
```python
import jax
import jax.numpy as jnp
from jax import lax
from jax.sharding import Mesh
from jax.sharding import PartitionSpec as P

REP = ("rep_0", "rep_1", "rep_2")


def sent_to_all(value, axis):
    count = lax.axis_size(axis)
    return lax.all_to_all(
        jnp.broadcast_to(value[None], (count, *value.shape)), axis, 0, 0, tiled=True
    )


def of_everyone(value, axis):
    everything = sent_to_all(value, axis)
    return jnp.sum(everything, axis=0)


def one_axis_at_a_time(value, axes):
    for axis in axes:
        value = lax.psum(value, axis)
    return value


def gathered_total(value, axis):
    pieces = lax.all_gather(value, axis)
    return pieces.sum(axis=0)


def body(inputs, cotangent, momentum, right_prev):
    high = lax.Precision.HIGHEST
    col_count = momentum.shape[1]
    out_total = cotangent.shape[1]
    in_total = col_count * lax.axis_size("shard")
    rank_size = right_prev.shape[1]
    gradient = lax.psum_scatter(
        lax.dot_general(
            cotangent, inputs, (((0,), (0,)), ((), ())), preferred_element_type=jnp.float32
        ),
        REP,
        scatter_dimension=0,
        tiled=True,
    )
    blended = momentum + gradient
    left_raw = of_everyone(jnp.dot(blended, right_prev, precision=high), "shard")
    gram_sum = one_axis_at_a_time(jnp.dot(left_raw.T, left_raw, precision=high), REP)
    lower_factor = jnp.linalg.cholesky(gram_sum)
    ortho = lax.linalg.triangular_solve(lower_factor, left_raw.T, left_side=True, lower=True).T
    local_right = jnp.dot(blended.T, ortho, precision=high)
    right_raw = gathered_total(local_right, REP)
    column_sq = of_everyone(jnp.sum(right_raw * right_raw, axis=0), "shard")
    new_momentum = blended - 0.05 * jnp.dot(ortho, right_raw.T, precision=high)
    right_factor = right_raw / jnp.sqrt(column_sq + 1e-06)
    scale_factor = (out_total * in_total / rank_size) ** 0.5
    update = (scale_factor * jnp.dot(ortho, right_factor.T, precision=high)).astype(jnp.bfloat16)
    return (new_momentum, right_factor, update)


def solution(mesh):
    finer = Mesh(
        mesh.devices.reshape(4, 12, 2, mesh.shape["shard"]), ("rep_0", "rep_1", "rep_2", "shard")
    )
    in_specs = (P(REP, "shard"), P(REP, None), P(REP, "shard"), P("shard", None))
    out_specs = (P(REP, "shard"), P("shard", None), P(REP, "shard"))
    return jax.shard_map(body, mesh=finer, in_specs=in_specs, out_specs=out_specs, check_vma=False)
```

profile of v0, /device:TPU:1, one launch (start us, length us, event | category | flops | bytes accessed | tf_op | source)
XLA Modules:
  0.0 471.4 jit_solution(6155839359900269903)
XLA Ops:
  7.2 0.0 copy-start
  7.2 0.0 copy-start.2
  7.2 0.0 copy-start.3
  7.2 0.0 reduce-scatter.2.cloned.1.call-start
  7.2 0.9 copy-done
  8.1 6.8 %fusion.6 = f32[6144,256]{1,0:T(8,128)} fusion(bf16[384,6144]{1,0:T(8,128)(2,1)} %param.5, bf16[384,256]{1,0:T(8,128)(2,1)S(1)} %copy-done), kind=kOutput, calls=%fused_computation.18 | convolution fusion | flops 1207959552 | bytes 11206656 | tf_op jit(solution)/shard_map/dot_general | solution.py:40
  14.9 0.0 reduce-scatter.2.cloned.1.call-update
  15.0 0.0 all-gather.3.cloned.1.call-start
  15.0 217.4 %reduce-scatter.2.cloned.1.call-done = f32[64,256]{1,0:T(8,128)} async-done(((f32[6144,256]{1,0:T(8,128)}), f32[64,256]{1,0:T(8,128)}) %reduce-scatter.2.cloned.1.call-update) | async-done | bytes 65552 | tf_op jit(solution)/shard_map/reduce_scatter | solution.py:39
  232.4 0.0 copy-done.2
  232.4 0.8 add.32
  233.2 0.0 copy-done.3
  233.3 0.2 fusion.7
  233.5 0.2 reshape.27
  233.7 14.2 %all_to_all.11 = f32[8,1,4096]{2,1,0:T(1,128)S(1)} all-to-all(f32[8,1,4096]{2,1,0:T(1,128)S(1)} %reshape.27), channel_id=1, replica_groups=mesh['rep_0'=4,'rep_1'=12,'rep_2'=2,'shard'=8] {'shard'}, dimensions={0} | all-to-all | bytes 262144 | tf_op jit(solution)/shard_map/all_to_all | solution.py:12
  247.9 0.5 broadcast.55
  248.4 1.0 reduce.7
  249.3 0.1 reshape.28
  249.5 0.2 fusion.8
  249.7 13.8 %psum.21 = f32[64,64]{0,1:T(8,128)S(1)} all-reduce(f32[64,64]{0,1:T(8,128)S(1)} %fusion.8), channel_id=1, replica_groups=mesh['rep_0'=4,'rep_1'=12,'rep_2'=2,'shard'=8] {'rep_0'}, use_global_device_ids=true, to_apply=%region_2.0 | all-reduce | flops 4096 | bytes 32768 | tf_op jit(solution)/shard_map/psum | solution.py:24
  263.5 30.5 %psum.22 = f32[64,64]{0,1:T(8,128)S(1)} all-reduce(f32[64,64]{0,1:T(8,128)S(1)} %psum.21), channel_id=1, replica_groups=mesh['rep_0'=4,'rep_1'=12,'rep_2'=2,'shard'=8] {'rep_1'}, use_global_device_ids=true, to_apply=%region_3.0 | all-reduce | flops 4096 | bytes 32768 | tf_op jit(solution)/shard_map/psum | solution.py:24
  294.0 27.2 %psum.23 = f32[64,64]{0,1:T(8,128)S(1)} all-reduce(f32[64,64]{0,1:T(8,128)S(1)} %psum.22), channel_id=1, replica_groups=mesh['rep_0'=4,'rep_1'=12,'rep_2'=2,'shard'=8] {'rep_2'}, use_global_device_ids=true, to_apply=%region_4.0 | all-reduce | flops 4096 | bytes 32768 | tf_op jit(solution)/shard_map/psum | solution.py:24
  321.2 0.1 copy.12
  321.3 5.8 %cholesky.16 = f32[64,64]{1,0:T(8,128)S(1)} custom-call(f32[64,64]{1,0:T(8,128)S(1)} %fusion.5), custom_call_target="Cholesky" | custom-call | tf_op jit(solution)/shard_map/jit(cholesky)/cholesky | solution.py:50
  327.2 0.6 compare_reduce_fusion
  327.8 0.7 fusion.2
  328.5 4.9 %custom-call.6 = f32[1,64,64]{1,2,0:T(8,128)S(1)} custom-call(f32[1,64,64]{2,1,0:T(8,128)S(1)} %fusion.2), custom_call_target="InvertDiagBlocksLowerTriangular" | custom-call | tf_op jit(solution)/shard_map/triangular_solve | solution.py:51
  333.4 0.2 fusion.3
  333.6 0.8 fusion.9
  334.4 0.0 all-gather.3.cloned.1.call-update
  334.5 109.6 %all-gather.3.cloned.1.call-done = f32[24576,64]{0,1:T(8,128)} async-done(((f32[256,64]{0,1:T(8,128)}), f32[24576,64]{0,1:T(8,128)}) %all-gather.3.cloned.1.call-update) | async-done | bytes 6291472 | tf_op jit(solution)/shard_map/all_gather | solution.py:29
  444.1 4.7 copy.15
  448.8 1.2 bitcast_reduce_fusion
  449.9 0.1 multiply_reduce_fusion
  450.0 0.6 broadcast_in_dim.7
  450.6 6.5 %all-to-all-start.1 = ((f32[8,1,64]{2,1,0:T(1,128)}), f32[8,1,64]{2,1,0:T(1,128)S(1)}, u32[]{:S(2)}, u32[]{:S(2)}) async-start(f32[8,1,64]{2,1,0:T(1,128)} %broadcast_in_dim.7), calls=%async_computation.2 | async-start | bytes 8192 | tf_op jit(solution)/shard_map/all_to_all | solution.py:12
  457.1 0.9 fusion
  458.0 5.6 %all-to-all-done.1 = f32[8,1,64]{2,1,0:T(1,128)S(1)} async-done(((f32[8,1,64]{2,1,0:T(1,128)}), f32[8,1,64]{2,1,0:T(1,128)S(1)}, u32[]{:S(2)}, u32[]{:S(2)}) %all-to-all-start.1) | async-done | bytes 2080 | tf_op jit(solution)/shard_map/all_to_all | solution.py:12
  463.6 0.1 broadcast_divide_fusion
  463.7 0.0 copy-start.1
  463.7 0.9 fusion.1
  464.6 0.0 copy-done.1
  (6 shorter events, 0.1 us)
Async XLA Ops:
  7.2 0.9 copy-start
  7.2 225.2 %copy-start.2 = (f32[64,256]{1,0:T(8,128)S(1)}, f32[64,256]{1,0:T(8,128)}, u32[]{:S(2)}) copy-start(f32[64,256]{1,0:T(8,128)} %param.6) | copy-start | bytes 196612
  7.2 226.1 %copy-start.3 = (f32[256,64]{0,1:T(8,128)S(1)}, f32[256,64]{0,1:T(8,128)}, u32[]{:S(2)}) copy-start(f32[256,64]{0,1:T(8,128)} %param.7) | copy-start | bytes 196612
  7.2 225.2 %reduce-scatter.2.cloned.1.call-start = ((), (), s32[]{:S(2)}) async-start(), calls=%async_computation.3 | async-start | bytes 6356992 | tf_op jit(solution)/shard_map/reduce_scatter | solution.py:39
  15.0 429.1 %all-gather.3.cloned.1.call-start = ((), (), s32[]{:S(2)}) async-start(), calls=%async_computation.4 | async-start | bytes 6356992 | tf_op jit(solution)/shard_map/all_gather | solution.py:29
  450.6 12.9 %all-to-all-start.1 = ((f32[8,1,64]{2,1,0:T(1,128)}), f32[8,1,64]{2,1,0:T(1,128)S(1)}, u32[]{:S(2)}, u32[]{:S(2)}) async-start(f32[8,1,64]{2,1,0:T(1,128)} %broadcast_in_dim.7), calls=%async_computation.2 | async-start | bytes 8192 | tf_op jit(solution)/shard_map/all_to_all | solution.py:12
  463.7 0.9 copy-start.1
Sparse Core Ops, SparseCore 0:
  15.1 217.2 reduce-scatter.1
  334.6 109.4 all-gather.2
where the time goes:
time: 472 us; the launch traced here: 471 us
  waiting for transfers between devices  333 us (71%)
  blocking collectives  85.6 us (18%)
  other arithmetic  15.3 us (3%)
  between operations  14.2 us (3%)
  matrix products  10.1 us (2%)
  local copies, waits for them, and re-layouts  7.03 us (1%)
  starting transfers between devices  6.54 us (1%)
    reduce_scatter x1, waiting for transfers between devices, body(): lax.psum_scatter(lax.dot_general(cotangent, inputs, (((0,), (0,)), ((), (...  217 us
    all_gather x1, waiting for transfers between devices, gathered_total(): pieces = lax.all_gather(value, axis)  110 us
    psum x3, blocking collectives, one_axis_at_a_time(): value = lax.psum(value, axis)  71.4 us
    all_to_all x1, blocking collectives, sent_to_all(): lax.all_to_all(jnp.broadcast_to(value[None], (count, *value.shape)), axis...  14.2 us
  transfers between devices with their start and end apart: 3, of which 3 were waited for; matrix products, arithmetic and copies ran while one was open for 0% of the time, Pallas kernels for 0%

commit v1 on v0

v1 whole, which is shorter than its diff:
```python
import jax
import jax.numpy as jnp
from jax import lax
from jax.sharding import Mesh
from jax.sharding import PartitionSpec as P

X, ZA, ZB, CORE, SHARD = "rep_x", "rep_za", "rep_zb", "rep_core", "shard"
REP = (X, ZA, ZB, CORE)
HIGH = lax.Precision.HIGHEST


def exchanged(pieces, axis):
    return lax.all_to_all(pieces, axis, 0, 0, tiled=True)


def scattered_sum(pieces, axis):
    return jnp.sum(exchanged(pieces, axis), axis=0)


def from_everyone(value, axis):
    count = lax.axis_size(axis)
    return exchanged(jnp.broadcast_to(value[None], (count, *value.shape)), axis)


def gradient_rows(inputs, cotangent):
    nx, na, nb = (lax.axis_size(a) for a in (X, ZA, ZB))
    partial = lax.dot_general(
        cotangent, inputs, (((0,), (0,)), ((), ())), preferred_element_type=jnp.float32
    )
    rows, cols = partial.shape[0] // (nx * na * nb * 2), partial.shape[1]
    halves = partial.reshape(nx * na * nb, 2, rows, cols)
    core = lax.axis_index(CORE)
    mine = lax.dynamic_index_in_dim(halves, core, 1, keepdims=False)
    other = lax.dynamic_index_in_dim(halves, 1 - core, 1, keepdims=False)
    chip = mine + lax.ppermute(other, CORE, ((0, 1), (1, 0)))
    over_x = scattered_sum(chip.reshape(nx, na * nb * rows, cols), X)
    by_zb = over_x.reshape(na, nb, rows, cols).transpose(1, 0, 2, 3)
    over_zb = scattered_sum(by_zb.reshape(nb, na * rows, cols), ZB)
    return scattered_sum(over_zb.reshape(na, rows, cols), ZA)


def rep_total(value):
    members = lax.axis_size((X, CORE))
    piece = scattered_sum(value.reshape(members, value.shape[0] // members, value.shape[1]), (X, CORE))
    piece = jnp.sum(from_everyone(piece, (ZA, ZB)), axis=0)
    return from_everyone(piece, (X, CORE)).reshape(value.shape)


def body(inputs, cotangent, momentum, right_prev):
    out_total = cotangent.shape[1]
    in_total = momentum.shape[1] * lax.axis_size(SHARD)
    rank = right_prev.shape[1]
    cols = momentum.shape[1]
    blended = momentum + gradient_rows(inputs, cotangent)
    left_part = jnp.dot(blended, right_prev, precision=HIGH)
    half = left_part.shape[0] // 2
    packed = jnp.concatenate([left_part[:half], left_part[half:]], axis=1)
    packed = jnp.sum(from_everyone(packed, SHARD), axis=0)
    left_raw = jnp.concatenate([packed[:, :rank], packed[:, rank:]], axis=0)
    both = jnp.concatenate([blended, left_raw, jnp.zeros_like(left_raw)], axis=1)
    total = rep_total(lax.dot_general(left_raw, both, (((0,), (0,)), ((), ())), precision=HIGH))
    projected, gram_sum = total[:, :cols], total[:, cols : cols + rank]
    lower_factor = jnp.linalg.cholesky(gram_sum)
    inverse = lax.linalg.triangular_solve(
        lower_factor, jnp.eye(rank, dtype=jnp.float32), left_side=True, lower=True
    )
    ortho = lax.dot_general(left_raw, inverse, (((1,), (1,)), ((), ())), precision=HIGH)
    right_rows = jnp.dot(inverse, projected, precision=HIGH)
    column_sq = jnp.sum(from_everyone(jnp.sum(right_rows * right_rows, axis=1), SHARD), axis=0)
    new_momentum = blended - 0.05 * jnp.dot(ortho, right_rows, precision=HIGH)
    factor_rows = right_rows / jnp.sqrt(column_sq + 1e-06)[:, None]
    scale_factor = (out_total * in_total / rank) ** 0.5
    update = (scale_factor * jnp.dot(ortho, factor_rows, precision=HIGH)).astype(jnp.bfloat16)
    return (new_momentum, factor_rows.T, update)


def solution(mesh):
    finer = Mesh(mesh.devices.reshape(4, 4, 3, 2, mesh.shape["shard"]), (*REP, SHARD))
    in_specs = (P(REP, SHARD), P(REP, None), P(REP, SHARD), P(SHARD, None))
    out_specs = (P(REP, SHARD), P(SHARD, None), P(REP, SHARD))
    return jax.shard_map(body, mesh=finer, in_specs=in_specs, out_specs=out_specs, check_vma=False)
```

time: 472 us -> 185 us (0.39)
  waiting for transfers between devices: 333 us -> 11 us
  blocking collectives: 85.6 us -> 126 us
  between operations: 14.2 us -> 0.82 us
  starting transfers between devices: 6.54 us -> 15.7 us
    reduce_scatter x1 -> x0, waiting for transfers between devices: 217 us -> none  [body(): lax.psum_scatter(lax.dot_general(cotangent, inputs, (((0,), (0,)), ((), (...]
    all_to_all x1 -> x7, blocking collectives: 14.2 us -> 126 us  [exchanged(): return lax.all_to_all(pieces, axis, 0, 0, tiled=True)]
    all_gather x1 -> x0, waiting for transfers between devices: 110 us -> none  [gathered_total(): pieces = lax.all_gather(value, axis)]
    psum x3 -> x0, blocking collectives: 71.4 us -> none  [one_axis_at_a_time(): value = lax.psum(value, axis)]
    ppermute x0 -> x1, starting transfers between devices: none -> 12.4 us  [gradient_rows(): chip = mine + lax.ppermute(other, CORE, ((0, 1), (1, 0)))]
    ppermute x0 -> x1, waiting for transfers between devices: none -> 5.4 us  [gradient_rows(): chip = mine + lax.ppermute(other, CORE, ((0, 1), (1, 0)))]
    dot_general x6 -> x7, matrix products: 9.86 us -> 6.88 us  [the longest x1 4.17 us: gradient_rows(): lax.dot_general(cotangent, inputs, (((0,), (0,)), ((), ())), preferred_el...]
  transfers between devices with their start and end apart: 3 -> 2, of which waited for: 3 -> 2; matrix products, arithmetic and copies ran while one was open for 0% -> 0% of each run, Pallas kernels for 0% -> 0%
where the time goes in v1:
time: 185 us; the launch traced here: 184 us
  blocking collectives  126 us (68%)
  other arithmetic  17.7 us (10%)
  starting transfers between devices  15.7 us (8%)
  waiting for transfers between devices  11 us (6%)
  matrix products  7.11 us (4%)
  local copies, waits for them, and re-layouts  5.9 us (3%)
    all_to_all x7, blocking collectives, exchanged(): return lax.all_to_all(pieces, axis, 0, 0, tiled=True)  126 us
    ppermute x1, starting transfers between devices, gradient_rows(): chip = mine + lax.ppermute(other, CORE, ((0, 1), (1, 0)))  12.4 us
    another operation x3, other arithmetic, body(): lower_factor = jnp.linalg.cholesky(gram_sum)  6.52 us
    all_to_all x1, waiting for transfers between devices, exchanged(): return lax.all_to_all(pieces, axis, 0, 0, tiled=True)  5.57 us
    another operation x2, other arithmetic, body(): lax.linalg.triangular_solve(lower_factor, jnp.eye(rank, dtype=jnp.float32...  5.55 us
    ppermute x1, waiting for transfers between devices, gradient_rows(): chip = mine + lax.ppermute(other, CORE, ((0, 1), (1, 0)))  5.4 us
    dot_general x1, matrix products, gradient_rows(): lax.dot_general(cotangent, inputs, (((0,), (0,)), ((), ())), preferred_el...  4.17 us
  transfers between devices with their start and end apart: 2, of which 2 were waited for; matrix products, arithmetic and copies ran while one was open for 0% of the time, Pallas kernels for 0%

profile of v1, /device:TPU:1, one launch (start us, length us, event | category | flops | bytes accessed | tf_op | source)
XLA Modules:
  0.0 184.3 jit_solution(13133351957521949637)
XLA Ops:
  0.6 0.0 copy-start
  0.7 0.9 copy-done
  1.6 4.2 %fusion.21 = f32[6144,256]{1,0:T(8,128)S(1)} fusion(bf16[384,6144]{1,0:T(8,128)(2,1)} %param.5, bf16[384,256]{1,0:T(8,128)(2,1)S(1)} %copy-done), kind=kOutput, calls=%fused_computation.37 | convolution fusion | flops 1207959552 | bytes 11206656 | tf_op jit(solution)/shard_map/dot_general | solution.py:27
  5.7 0.0 copy-start.1
  5.8 2.7 %copy-done.1 = f32[6144,256]{1,0:T(8,128)} copy-done((f32[6144,256]{1,0:T(8,128)}, f32[6144,256]{1,0:T(8,128)S(1)}, u32[]{:S(2)}) %copy-start.1) | copy-done | bytes 6291480
  8.4 0.3 dynamic-slice_bitcast_fusion
  8.8 12.4 %collective-permute-start = (f32[48,64,256]{2,1,0:T(8,128)S(1)}, f32[48,64,256]{2,1,0:T(8,128)}, u32[]{:S(2)}, u32[]{:S(2)}) collective-permute-start(f32[48,64,256]{2,1,0:T(8,128)S(1)} %dynamic-slice_bitcast_fusion), channel_id=1, source_target_pairs={{0,8},{8,0},{1,9},{9,1},{2,10},{10,2},{3,11},{11,3},{4,12},{12,4},... | collective-permute-start | bytes 9437192 | tf_op jit(solution)/shard_map/ppermute | solution.py:35
  21.2 5.4 %collective-permute-done = f32[48,64,256]{2,1,0:T(8,128)} collective-permute-done((f32[48,64,256]{2,1,0:T(8,128)S(1)}, f32[48,64,256]{2,1,0:T(8,128)}, u32[]{:S(2)}, u32[]{:S(2)}) %collective-permute-start) | collective-permute-done | bytes 3145760 | tf_op jit(solution)/shard_map/ppermute | solution.py:35
  26.6 3.5 %bitcast_add_fusion = f32[48,64,256]{2,1,0:T(8,128)S(1)} fusion(f32[48,64,256]{2,1,0:T(8,128)} %collective-permute-done, f32[48,2,64,256]{3,2,1,0:T(8,128)} %bitcast.36, s32[]{:T(128)S(6)} %select_n.11), kind=kLoop, calls=%fused_computation | loop fusion | flops 786432 | bytes 9437188 | tf_op jit(solution)/shard_map/add | solution.py:35
  30.1 39.8 %all_to_all.41 = f32[4,768,256]{2,1,0:T(8,128)S(1)} all-to-all(f32[4,768,256]{2,1,0:T(8,128)S(1)} %bitcast.37), channel_id=1, replica_groups=mesh['rep_x'=4,'rep_za'=4,'rep_zb'=3,'rep_core'=2,'shard'=8] {'rep_x'}, dimensions={0} | all-to-all | bytes 6291456 | tf_op jit(solution)/shard_map/all_to_all | solution.py:13
  69.9 0.0 copy-start.2
  69.9 0.0 copy-start.3
  69.9 1.1 reduce_sum.72
  71.0 1.2 copy.16
  72.2 15.1 %all_to_all.42 = f32[3,256,256]{2,1,0:T(8,128)S(1)} all-to-all(f32[3,256,256]{2,1,0:T(8,128)S(1)} %bitcast.38), channel_id=1, replica_groups=mesh['rep_x'=4,'rep_za'=4,'rep_zb'=3,'rep_core'=2,'shard'=8] {'rep_zb'}, dimensions={0} | all-to-all | bytes 1572864 | tf_op jit(solution)/shard_map/all_to_all | solution.py:13
  87.3 0.1 reduce_sum.73
  87.4 19.7 %all_to_all.43 = f32[4,64,256]{2,1,0:T(8,128)S(1)} all-to-all(f32[4,64,256]{2,1,0:T(8,128)S(1)} %bitcast.40), channel_id=1, replica_groups=mesh['rep_x'=4,'rep_za'=4,'rep_zb'=3,'rep_core'=2,'shard'=8] {'rep_za'}, dimensions={0} | all-to-all | bytes 524288 | tf_op jit(solution)/shard_map/all_to_all | solution.py:13
  107.1 0.0 copy-done.2
  107.1 0.0 copy-done.3
  107.1 0.2 fusion.22
  107.4 0.1 pad_maximum_fusion.3
  107.5 14.5 %all_to_all.44 = f32[8,32,128]{2,1,0:T(8,128)S(1)} all-to-all(f32[8,32,128]{2,1,0:T(8,128)S(1)} %broadcast_in_dim.11), channel_id=1, replica_groups=mesh['rep_x'=4,'rep_za'=4,'rep_zb'=3,'rep_core'=2,'shard'=8] {'shard'}, dimensions={0} | all-to-all | bytes 262144 | tf_op jit(solution)/shard_map/all_to_all | solution.py:13
  122.0 0.1 fusion.20
  122.1 0.3 convolution_bitcast_fusion
  122.4 12.5 %all_to_all.45 = f32[8,8,384]{2,1,0:T(8,128)S(1)} all-to-all(f32[8,8,384]{2,1,0:T(8,128)S(1)} %convolution_bitcast_fusion), channel_id=1, replica_groups=mesh['rep_x'=4,'rep_za'=4,'rep_zb'=3,'rep_core'=2,'shard'=8] {'rep_x','r..., dimensions={0} | all-to-all | bytes 196608 | tf_op jit(solution)/shard_map/all_to_all | solution.py:13
  135.0 14.3 %all_to_all.46 = f32[12,8,384]{2,1,0:T(8,128)S(1)} all-to-all(f32[12,8,384]{2,1,0:T(8,128)S(1)} %broadcast_in_dim.13), channel_id=1, replica_groups=mesh['rep_x'=4,'rep_za'=4,'rep_zb'=3,'rep_core'=2,'shard'=8] {'rep_za','..., dimensions={0} | all-to-all | bytes 294912 | tf_op jit(solution)/shard_map/all_to_all | solution.py:13
  149.3 10.2 %all_to_all.47 = f32[8,8,384]{2,1,0:T(8,128)S(1)} all-to-all(f32[8,8,384]{2,1,0:T(8,128)S(1)} %broadcast_in_dim.15), channel_id=1, replica_groups=mesh['rep_x'=4,'rep_za'=4,'rep_zb'=3,'rep_core'=2,'shard'=8] {'rep_x','r..., dimensions={0} | all-to-all | bytes 196608 | tf_op jit(solution)/shard_map/all_to_all | solution.py:13
  159.5 0.1 copy.20
  159.6 5.8 %cholesky.16 = f32[64,64]{1,0:T(8,128)S(1)} custom-call(f32[64,64]{1,0:T(8,128)S(1)} %fusion.15), custom_call_target="Cholesky" | custom-call | tf_op jit(solution)/shard_map/jit(cholesky)/cholesky | solution.py:63
  165.5 0.6 compare_reduce_fusion
  166.1 0.7 fusion.11
  166.8 4.9 %custom-call.6 = f32[1,64,64]{1,2,0:T(8,128)S(1)} custom-call(f32[1,64,64]{2,1,0:T(8,128)S(1)} %fusion.11), custom_call_target="InvertDiagBlocksLowerTriangular" | custom-call | tf_op jit(solution)/shard_map/triangular_solve | solution.py:64
  171.7 0.2 fusion.13
  171.9 0.3 multiply_reduce_fusion
  172.2 0.2 fusion.12
  172.4 0.6 broadcast_in_dim.16
  173.0 3.3 %all-to-all-start.7 = ((f32[8,1,64]{2,1,0:T(1,128)}), f32[8,1,64]{2,1,0:T(1,128)S(1)}, u32[]{:S(2)}, u32[]{:S(2)}) async-start(f32[8,1,64]{2,1,0:T(1,128)} %broadcast_in_dim.16), calls=%async_computation.7 | async-start | bytes 8192 | tf_op jit(solution)/shard_map/all_to_all | solution.py:13
  176.3 0.8 fusion
  177.1 5.6 %all-to-all-done.7 = f32[8,1,64]{2,1,0:T(1,128)S(1)} async-done(((f32[8,1,64]{2,1,0:T(1,128)}), f32[8,1,64]{2,1,0:T(1,128)S(1)}, u32[]{:S(2)}, u32[]{:S(2)}) %all-to-all-start.7) | async-done | bytes 2080 | tf_op jit(solution)/shard_map/all_to_all | solution.py:13
  182.7 0.9 fusion.1
  183.6 0.7 fusion.16
  (15 shorter events, 0.2 us)
Async XLA Ops:
  0.6 0.9 copy-start
  5.7 2.7 %copy-start.1 = (f32[6144,256]{1,0:T(8,128)}, f32[6144,256]{1,0:T(8,128)S(1)}, u32[]{:S(2)}) copy-start(f32[6144,256]{1,0:T(8,128)S(1)} %fusion.21) | copy-start | bytes 18874372
  8.8 17.8 %collective-permute-start = (f32[48,64,256]{2,1,0:T(8,128)S(1)}, f32[48,64,256]{2,1,0:T(8,128)}, u32[]{:S(2)}, u32[]{:S(2)}) collective-permute-start(f32[48,64,256]{2,1,0:T(8,128)S(1)} %dynamic-slice_bitcast_fusion), channel_id=1, source_target_pairs={{0,8},{8,0},{1,9},{9,1},{2,10},{10,2},{3,11},{11,3},{4,12},{12,4},... | collective-permute-start | bytes 9437192 | tf_op jit(solution)/shard_map/ppermute | solution.py:35
  69.9 37.2 %copy-start.2 = (f32[64,256]{1,0:T(8,128)S(1)}, f32[64,256]{1,0:T(8,128)}, u32[]{:S(2)}) copy-start(f32[64,256]{1,0:T(8,128)} %param.6) | copy-start | bytes 196612
  69.9 37.2 %copy-start.3 = (f32[256,64]{0,1:T(8,128)S(1)}, f32[256,64]{0,1:T(8,128)}, u32[]{:S(2)}) copy-start(f32[256,64]{0,1:T(8,128)} %param.7) | copy-start | bytes 196612
  173.0 9.7 %all-to-all-start.7 = ((f32[8,1,64]{2,1,0:T(1,128)}), f32[8,1,64]{2,1,0:T(1,128)S(1)}, u32[]{:S(2)}, u32[]{:S(2)}) async-start(f32[8,1,64]{2,1,0:T(1,128)} %broadcast_in_dim.16), calls=%async_computation.7 | async-start | bytes 8192 | tf_op jit(solution)/shard_map/all_to_all | solution.py:13

commit v2 on v1

v2 whole, which is shorter than its diff:
```python
import functools

import jax
import jax.numpy as jnp
from jax import lax
from jax.experimental import pallas as pl
from jax.experimental.pallas import tpu as pltpu
from jax.sharding import Mesh
from jax.sharding import PartitionSpec as P

X, Z, CORE, SHARD = "rep_x", "rep_z", "rep_core", "shard"
REP = (X, Z, CORE)
CLASSES = 3
HIGH = lax.Precision.HIGHEST


def exchanged(pieces, axis, groups=None):
    return lax.all_to_all(pieces, axis, 0, 0, tiled=True, axis_index_groups=groups)


def from_everyone(value, axis):
    count = lax.axis_size(axis)
    return exchanged(jnp.broadcast_to(value[None], (count, *value.shape)), axis)


def sent(value, axis, distance):
    size = lax.axis_size(axis)
    return lax.ppermute(value, axis, [(i, (i + distance) % size) for i in range(size)])


def gated(value, *earlier):
    return lax.optimization_barrier((value, *earlier))[0]


def gradient_rows(inputs, cotangent):
    nx, nz = lax.axis_size(X), lax.axis_size(Z)
    na, nb = nz // CLASSES, CLASSES
    cols = inputs.shape[1]
    rows = cotangent.shape[1] // (nx * nz * 2)
    x, z, core = lax.axis_index(X), lax.axis_index(Z), lax.axis_index(CORE)
    half = na // 2

    partial = lax.dot_general(
        cotangent, inputs, (((0,), (0,)), ((), ())), preferred_element_type=jnp.float32
    ).reshape(nx, na, nb, 2, rows, cols)

    def piece(ahead, which):
        at_x = lax.dynamic_index_in_dim(partial, (x + ahead) % nx, 0, keepdims=False)
        return lax.dynamic_index_in_dim(at_x, which, 2, keepdims=False)

    far = sent(piece(2, 1 - core), CORE, 1)
    near = jnp.stack([piece(ahead, 1 - core) for ahead in (1, 3, 0)])
    near = sent(near, CORE, 1)
    mine = piece(2, core)
    far_up, far_down = mine[:half] + far[:half], mine[half:] + far[half:]
    relay_up = sent(far_up, X, 1)
    relay_down = sent(far_down, X, -1)
    near = gated(near, far_up, far_down)
    before, after = piece(1, core), piece(3, core)
    before_low, before_high = before[:half] + near[0, :half], before[half:] + near[0, half:]
    after_low, after_high = after[:half] + near[1, :half], after[half:] + near[1, half:]
    high_below = sent(before_high, X, 1)
    low_above = sent(after_low, X, -1)
    relay_up = gated(relay_up, before_low, before_high, after_low)
    low_below = sent(before_low + relay_up, X, 1)
    relay_down = gated(relay_down, after_high, before_high, after_low)
    high_above = sent(after_high + relay_down, X, -1)
    own = lax.optimization_barrier(piece(0, core) + near[2])
    low = own[:half] + low_below + low_above
    high = own[half:] + high_below + high_above
    over_x = jnp.concatenate([low, high], axis=0)

    kind = z % nb

    def of_class(ahead):
        return lax.dynamic_index_in_dim(over_x, (kind + ahead) % nb, 1, keepdims=False)

    up = sent(of_class(1), Z, 1)
    down = sent(of_class(nb - 1), Z, -1)
    over_near_z = of_class(0) + up + down
    groups = [[a * nb + b for a in range(na)] for b in range(nb)]
    return exchanged(over_near_z, Z, groups)


def rep_total(value):
    members = lax.axis_size((X, CORE))
    piece = value.reshape(members, value.shape[0] // members, value.shape[1])
    piece = jnp.sum(exchanged(piece, (X, CORE)), axis=0)
    piece = jnp.sum(from_everyone(piece, Z), axis=0)
    return from_everyone(piece, (X, CORE)).reshape(value.shape)


def eliminate(total_ref, left_ref, ortho_ref, right_ref, squares_ref):
    rank = left_ref.shape[1]
    cols = right_ref.shape[1]
    tile = 8
    wide = 2 * rank
    full = total_ref[:, cols : cols + wide]
    row = lax.broadcasted_iota(jnp.int32, (rank, wide), 0)
    lane = lax.broadcasted_iota(jnp.int32, (rank, wide), 1)
    diagonal = jnp.where(lane == row, full, 0.0)
    down = lax.rsqrt(jnp.sum(diagonal, axis=1, keepdims=True))
    along = lax.rsqrt(jnp.sum(diagonal + jnp.where(lane == row + rank, 1.0, 0.0), axis=0, keepdims=True))
    scaled = jnp.where(lane < rank, full * down * along, jnp.where(lane == row + rank, down, 0.0))
    blocks = [scaled[b * tile : (b + 1) * tile, :] for b in range(rank // tile)]
    row_of = lax.broadcasted_iota(jnp.int32, (tile, wide), 0)
    for k in range(0, rank, 2):
        b, r = divmod(k, tile)
        first, second = blocks[b][r : r + 1, :], blocks[b][r + 1 : r + 2, :]
        a, c, d = first[:, k : k + 1], first[:, k + 1 : k + 2], second[:, k + 1 : k + 2]
        det = a * d - c * c
        inv = 1.0 / det
        to_first = (d * inv) * first - (c * inv) * second
        to_second = (a * inv) * second - (c * inv) * first
        unit_first = first * lax.rsqrt(a)
        unit_second = (second - (c / a) * first) * lax.rsqrt(det / a)
        for i in range(b, rank // tile):
            old = blocks[i]
            new = old - old[:, k : k + 1] * to_first - old[:, k + 1 : k + 2] * to_second
            if i == b:
                new = jnp.where(row_of > r + 1, new, old)
                new = jnp.where(row_of == r, unit_first, new)
                new = jnp.where(row_of == r + 1, unit_second, new)
            blocks[i] = new
    inverse = jnp.concatenate(blocks, axis=0)[:, rank:]
    ortho_ref[...] = lax.dot_general(
        left_ref[...], inverse, (((1,), (1,)), ((), ())), precision=HIGH,
        preferred_element_type=jnp.float32,
    )
    right = jnp.dot(
        inverse, total_ref[:, :cols], precision=HIGH, preferred_element_type=jnp.float32
    )
    right_ref[...] = right
    squares = lax.dot_general(
        jnp.ones((tile, cols), jnp.float32), right * right, (((1,), (1,)), ((), ())),
        precision=HIGH, preferred_element_type=jnp.float32,
    )
    squares = jnp.concatenate([squares, squares], axis=1)
    for i in range(squares_ref.shape[0]):
        squares_ref[i] = squares


def finish(ortho_ref, right_ref, squares_ref, factor_ref, update_ref, *, scale):
    rank = ortho_ref.shape[1]
    squares = squares_ref[0]
    for i in range(1, squares_ref.shape[0]):
        squares = squares + squares_ref[i]
    root = jnp.sqrt(squares[:1, :rank] + 1e-06)
    row = lax.broadcasted_iota(jnp.int32, (rank, rank), 0)
    lane = lax.broadcasted_iota(jnp.int32, (rank, rank), 1)
    root = jnp.sum(jnp.where(row == lane, root, 0.0), axis=1, keepdims=True)
    factor = right_ref[...] / root
    factor_ref[...] = factor
    update = jnp.dot(ortho_ref[...], factor, precision=HIGH, preferred_element_type=jnp.float32)
    update_ref[...] = (scale * update).astype(update_ref.dtype)


def local_kernel(kernel, *out_shapes):
    return pl.pallas_call(
        kernel,
        out_shape=out_shapes,
        compiler_params=pltpu.CompilerParams(vmem_limit_bytes=4 * 1024 * 1024),
    )


def body(inputs, cotangent, momentum, right_prev):
    out_total = cotangent.shape[1]
    shards = lax.axis_size(SHARD)
    in_total = momentum.shape[1] * shards
    rank = right_prev.shape[1]
    rows, cols = momentum.shape
    blended = momentum + jnp.sum(gradient_rows(inputs, cotangent), axis=0)
    left_part = jnp.dot(blended, right_prev, precision=HIGH)
    packed = jnp.concatenate([left_part[: rows // 2], left_part[rows // 2 :]], axis=1)
    packed = jnp.sum(from_everyone(packed, SHARD), axis=0)
    left_raw = jnp.concatenate([packed[:, :rank], packed[:, rank:]], axis=0)
    both = jnp.concatenate([blended, left_raw, jnp.zeros_like(left_raw)], axis=1)
    total = rep_total(lax.dot_general(left_raw, both, (((0,), (0,)), ((), ())), precision=HIGH))
    f32 = functools.partial(jax.ShapeDtypeStruct, dtype=jnp.float32)
    ortho, right_rows, squares = local_kernel(
        eliminate, f32((rows, rank)), f32((rank, cols)), f32((shards, 8, 2 * rank))
    )(total, left_raw)
    squares = exchanged(squares, SHARD)
    new_momentum = blended - 0.05 * jnp.dot(ortho, right_rows, precision=HIGH)
    scale = (out_total * in_total / rank) ** 0.5
    factor_rows, update = local_kernel(
        functools.partial(finish, scale=scale),
        f32((rank, cols)), jax.ShapeDtypeStruct((rows, cols), jnp.bfloat16),
    )(ortho, right_rows, squares)
    return (new_momentum, factor_rows.T, update)


def solution(mesh):
    finer = Mesh(mesh.devices.reshape(4, 12, 2, mesh.shape["shard"]), (*REP, SHARD))
    in_specs = (P(REP, SHARD), P(REP, None), P(REP, SHARD), P(SHARD, None))
    out_specs = (P(REP, SHARD), P(SHARD, None), P(REP, SHARD))
    return jax.shard_map(body, mesh=finer, in_specs=in_specs, out_specs=out_specs, check_vma=False)
```

time: 185 us -> 172 us (0.930)
  blocking collectives: 126 us -> 49.2 us
  starting transfers between devices: 15.7 us -> 56.1 us
  waiting for transfers between devices: 11 us -> 38.9 us
  other arithmetic: 17.7 us -> 5.58 us
  Pallas kernels: 0 us -> 9.4 us
    all_to_all x7 -> x3, blocking collectives: 126 us -> 49.2 us  [exchanged(): lax.all_to_all(pieces, axis, 0, 0, tiled=True, axis_index_groups=groups)]
    ppermute x1 -> x10, starting transfers between devices: 12.4 us -> 39.9 us  [sent(): lax.ppermute(value, axis, [(i, (i + distance) % size) for i in range(size)])]
    ppermute x1 -> x10, waiting for transfers between devices: 5.4 us -> 20.1 us  [sent(): lax.ppermute(value, axis, [(i, (i + distance) % size) for i in range(size)])]
    all_to_all x1 -> x3, waiting for transfers between devices: 5.57 us -> 18.8 us  [exchanged(): lax.all_to_all(pieces, axis, 0, 0, tiled=True, axis_index_groups=groups)]
    all_to_all x1 -> x3, starting transfers between devices: 3.31 us -> 16.1 us  [exchanged(): lax.all_to_all(pieces, axis, 0, 0, tiled=True, axis_index_groups=groups)]
    another operation x5 -> x1, other arithmetic: 12.1 us -> 0.15 us  [gradient_rows(): near = jnp.stack([piece(ahead, 1 - core) for ahead in (1, 3, 0)])]
    pallas_call x0 -> x2, Pallas kernels: none -> 9.4 us  [the longest x1 8.49 us: body(): local_kernel(eliminate, f32((rows, rank)), f32((rank, cols)), f32((shards...]
    add x2 -> x8, other arithmetic: 3.54 us -> 5.25 us  [the longest x1 1.93 us: gradient_rows(): after[half:] + near[1, half:]]
  transfers between devices with their start and end apart: 2 -> 13, of which waited for: 2 -> 8; matrix products, arithmetic and copies ran while one was open for 0% -> 3% of each run, Pallas kernels for 0% -> 0%
where the time goes in v2:
time: 172 us; the launch traced here: 171 us
  starting transfers between devices  56.1 us (33%)
  blocking collectives  49.2 us (29%)
  waiting for transfers between devices  38.9 us (23%)
  Pallas kernels  9.4 us (5%)
  other arithmetic  5.58 us (3%)
  matrix products  5.51 us (3%)
  local copies, waits for them, and re-layouts  5.16 us (3%)
    all_to_all x3, blocking collectives, exchanged(): lax.all_to_all(pieces, axis, 0, 0, tiled=True, axis_index_groups=groups)  49.2 us
    ppermute x10, starting transfers between devices, sent(): lax.ppermute(value, axis, [(i, (i + distance) % size) for i in range(size)])  39.9 us
    ppermute x10, waiting for transfers between devices, sent(): lax.ppermute(value, axis, [(i, (i + distance) % size) for i in range(size)])  20.1 us
    all_to_all x3, waiting for transfers between devices, exchanged(): lax.all_to_all(pieces, axis, 0, 0, tiled=True, axis_index_groups=groups)  18.8 us
    all_to_all x3, starting transfers between devices, exchanged(): lax.all_to_all(pieces, axis, 0, 0, tiled=True, axis_index_groups=groups)  16.1 us
    pallas_call x1, Pallas kernels, body(): local_kernel(eliminate, f32((rows, rank)), f32((rank, cols)), f32((shards...  8.49 us
    dot_general x1, matrix products, gradient_rows(): lax.dot_general(cotangent, inputs, (((0,), (0,)), ((), ())), preferred_el...  4.17 us
  transfers between devices with their start and end apart: 13, of which 8 were waited for; matrix products, arithmetic and copies ran while one was open for 3% of the time, Pallas kernels for 0%

profile of v2, /device:TPU:1, one launch (start us, length us, event | category | flops | bytes accessed | tf_op | source)
XLA Modules:
  0.0 170.9 jit_solution(12082973512942611172)
XLA Ops:
  0.6 0.0 copy-start
  0.7 0.8 copy-done
  1.6 4.2 %fusion.25 = f32[6144,256]{1,0:T(8,128)S(1)} fusion(bf16[384,6144]{1,0:T(8,128)(2,1)} %param.5, bf16[384,256]{1,0:T(8,128)(2,1)S(1)} %copy-done), kind=kOutput, calls=%fused_computation.52 | convolution fusion | flops 1207959552 | bytes 11206656 | tf_op jit(solution)/shard_map/dot_general | solution.py:43
  5.7 0.0 copy-start.1
  5.8 1.6 dynamic-slice_bitcast_fusion.1
  7.4 0.2 pad_maximum_fusion
  7.5 1.2 copy-done.1
  8.7 12.4 %collective-permute-start = (f32[3,4,3,64,256]{4,3,2,1,0:T(8,128)S(1)}, f32[3,4,3,64,256]{4,3,2,1,0:T(8,128)}, u32[]{:S(2)}, u32[]{:S(2)}) collective-permute-start(f32[3,4,3,64,256]{4,3,2,1,0:T(8,128)S(1)} %pad_maximum_fusion), channel_id=1, source_target_pairs={{0,8},{8,0},{1,9},{9,1},{2,10},{10,2},{3,11},{11,3},{4,12},{12,4},... | collective-permute-start | bytes 7077896 | tf_op jit(solution)/shard_map/ppermute | solution.py:28
  21.1 1.9 %collective-permute-start.1 = (f32[4,3,64,256]{3,2,1,0:T(8,128)}, f32[4,3,64,256]{3,2,1,0:T(8,128)}, u32[]{:S(2)}, u32[]{:S(2)}) collective-permute-start(f32[4,3,64,256]{3,2,1,0:T(8,128)} %get-tuple-element.24), channel_id=1, source_target_pairs={{0,8},{8,0},{1,9},{9,1},{2,10},{10,2},{3,11},{11,3},{4,12},{12,4},... | collective-permute-start | bytes 2359304 | tf_op jit(solution)/shard_map/ppermute | solution.py:28
  23.0 3.5 %collective-permute-done.1 = f32[4,3,64,256]{3,2,1,0:T(8,128)} collective-permute-done((f32[4,3,64,256]{3,2,1,0:T(8,128)}, f32[4,3,64,256]{3,2,1,0:T(8,128)}, u32[]{:S(2)}, u32[]{:S(2)}) %collective-permute-start.1) | collective-permute-done | bytes 786464 | tf_op jit(solution)/shard_map/ppermute | solution.py:28
  26.5 1.5 slice_add_fusion.2
  28.0 1.9 %collective-permute-start.2 = (f32[2,3,64,256]{3,2,1,0:T(8,128)S(1)}, f32[2,3,64,256]{3,2,1,0:T(8,128)S(1)}, u32[]{:S(2)}, u32[]{:S(2)}) collective-permute-start(f32[2,3,64,256]{3,2,1,0:T(8,128)S(1)} %get-tuple-element.23), channel_id=1, source_target_pairs={{0,192},{192,384},{384,576},{576,0},{1,193},{193,385},{385,577},{5... | collective-permute-start | bytes 1179656 | tf_op jit(solution)/shard_map/ppermute | solution.py:28
  29.9 4.6 %collective-permute-start.6 = (f32[2,3,64,256]{3,2,1,0:T(8,128)S(1)}, f32[2,3,64,256]{3,2,1,0:T(8,128)S(1)}, u32[]{:S(2)}, u32[]{:S(2)}) collective-permute-start(f32[2,3,64,256]{3,2,1,0:T(8,128)S(1)} %get-tuple-element.22), channel_id=1, source_target_pairs={{0,576},{192,0},{384,192},{576,384},{1,577},{193,1},{385,193},{577... | collective-permute-start | bytes 1179656 | tf_op jit(solution)/shard_map/ppermute | solution.py:28
  34.5 0.0 collective-permute-done
  34.5 1.9 %fusion.1 = (f32[2,3,64,256]{3,2,1,0:T(8,128)S(1)}, f32[2,3,64,256]{3,2,1,0:T(8,128)S(1)}, f32[2,3,64,256]{3,2,1,0:T(8,128)S(1)}, f32[2,3,64,256]{3,2,1,0:T(8,128)S(1)}) fusion(f32[4,4,3,2,64,256]{5,4,3,2,1,0:T(8,128)} %bitcast.80, s32[]{:T(128)S(6)} %select_n.107, s32[]{:T(128)S(6)} %add.222, s32[]{:T(128)S(6)} %select_n.99, ...), kind=kLoop, calls=%fused_computation.17 | loop fusion | flops 393216 | bytes 4718608 | tf_op jit(solution)/shard_map/add | solution.py:61
  36.4 4.9 %collective-permute-done.2 = f32[2,3,64,256]{3,2,1,0:T(8,128)S(1)} collective-permute-done((f32[2,3,64,256]{3,2,1,0:T(8,128)S(1)}, f32[2,3,64,256]{3,2,1,0:T(8,128)S(1)}, u32[]{:S(2)}, u32[]{:S(2)}) %collective-permute-start.2) | collective-permute-done | bytes 393248 | tf_op jit(solution)/shard_map/ppermute | solution.py:28
  41.4 0.1 add.203
  41.4 1.9 %collective-permute-start.3 = (f32[2,3,64,256]{3,2,1,0:T(8,128)S(1)}, f32[2,3,64,256]{3,2,1,0:T(8,128)S(1)}, u32[]{:S(2)}, u32[]{:S(2)}) collective-permute-start(f32[2,3,64,256]{3,2,1,0:T(8,128)S(1)} %add.203), channel_id=1, source_target_pairs={{0,192},{192,384},{384,576},{576,0},{1,193},{193,385},{385,577},{5... | collective-permute-start | bytes 1179656 | tf_op jit(solution)/shard_map/ppermute | solution.py:28
  43.3 0.0 collective-permute-done.6
  43.4 0.1 add.208
  43.4 0.0 copy-start.2
  43.4 4.7 %collective-permute-start.7 = (f32[2,3,64,256]{3,2,1,0:T(8,128)S(1)}, f32[2,3,64,256]{3,2,1,0:T(8,128)S(1)}, u32[]{:S(2)}, u32[]{:S(2)}) collective-permute-start(f32[2,3,64,256]{3,2,1,0:T(8,128)S(1)} %add.208), channel_id=1, source_target_pairs={{0,576},{192,0},{384,192},{576,384},{1,577},{193,1},{385,193},{577... | collective-permute-start | bytes 1179656 | tf_op jit(solution)/shard_map/ppermute | solution.py:28
  48.1 1.9 %collective-permute-start.4 = (f32[2,3,64,256]{3,2,1,0:T(8,128)S(1)}, f32[2,3,64,256]{3,2,1,0:T(8,128)S(1)}, u32[]{:S(2)}, u32[]{:S(2)}) collective-permute-start(f32[2,3,64,256]{3,2,1,0:T(8,128)S(1)} %get-tuple-element.29), channel_id=1, source_target_pairs={{0,576},{192,0},{384,192},{576,384},{1,577},{193,1},{385,193},{577... | collective-permute-start | bytes 1179656 | tf_op jit(solution)/shard_map/ppermute | solution.py:28
  50.1 3.4 %collective-permute-start.5 = (f32[2,3,64,256]{3,2,1,0:T(8,128)S(1)}, f32[2,3,64,256]{3,2,1,0:T(8,128)S(1)}, u32[]{:S(2)}, u32[]{:S(2)}) collective-permute-start(f32[2,3,64,256]{3,2,1,0:T(8,128)S(1)} %get-tuple-element.21), channel_id=1, source_target_pairs={{0,192},{192,384},{384,576},{576,0},{1,193},{193,385},{385,577},{5... | collective-permute-start | bytes 1179656 | tf_op jit(solution)/shard_map/ppermute | solution.py:28
  53.5 0.0 copy-start.3
  53.5 1.5 bitcast_add_fusion
  55.1 0.0 collective-permute-done.3
  55.1 0.0 collective-permute-done.7
  55.1 8.4 %collective-permute-done.4 = f32[2,3,64,256]{3,2,1,0:T(8,128)S(1)} collective-permute-done((f32[2,3,64,256]{3,2,1,0:T(8,128)S(1)}, f32[2,3,64,256]{3,2,1,0:T(8,128)S(1)}, u32[]{:S(2)}, u32[]{:S(2)}) %collective-permute-start.4) | collective-permute-done | bytes 393248 | tf_op jit(solution)/shard_map/ppermute | solution.py:28
  63.5 0.0 collective-permute-done.5
  63.5 0.2 fusion.2
  63.7 1.9 %collective-permute-start.8 = (f32[4,64,256]{2,1,0:T(8,128)S(1)}, f32[4,64,256]{2,1,0:T(8,128)S(1)}, u32[]{:S(2)}, u32[]{:S(2)}) collective-permute-start(f32[4,64,256]{2,1,0:T(8,128)S(1)} %get-tuple-element.30), channel_id=1, source_target_pairs={{0,16},{16,32},{32,48},{48,64},{64,80},{80,96},{96,112},{112,128},... | collective-permute-start | bytes 786440 | tf_op jit(solution)/shard_map/ppermute | solution.py:28
  65.7 5.3 %collective-permute-start.9 = (f32[4,64,256]{2,1,0:T(8,128)S(1)}, f32[4,64,256]{2,1,0:T(8,128)S(1)}, u32[]{:S(2)}, u32[]{:S(2)}) collective-permute-start(f32[4,64,256]{2,1,0:T(8,128)S(1)} %get-tuple-element.31), channel_id=1, source_target_pairs={{0,176},{16,0},{32,16},{48,32},{64,48},{80,64},{96,80},{112,96},{1... | collective-permute-start | bytes 786440 | tf_op jit(solution)/shard_map/ppermute | solution.py:28
  71.0 2.4 %collective-permute-done.8 = f32[4,64,256]{2,1,0:T(8,128)S(1)} collective-permute-done((f32[4,64,256]{2,1,0:T(8,128)S(1)}, f32[4,64,256]{2,1,0:T(8,128)S(1)}, u32[]{:S(2)}, u32[]{:S(2)}) %collective-permute-start.8) | collective-permute-done | bytes 262176 | tf_op jit(solution)/shard_map/ppermute | solution.py:28
  73.4 0.9 collective-permute-done.9
  74.3 0.1 fusion.12
  74.3 17.1 %all_to_all.30 = f32[4,64,256]{2,1,0:T(8,128)S(1)} all-to-all(f32[4,64,256]{2,1,0:T(8,128)S(1)} %fusion.12), channel_id=1, replica_groups={{0,48,96,144},{16,64,112,160},{32,80,128,176},{1,49,97,145},{17,65,113,..., dimensions={0} | all-to-all | bytes 524288 | tf_op jit(solution)/shard_map/all_to_all | solution.py:18
  91.4 0.0 copy-done.2
  91.4 0.0 copy-done.3
  91.5 0.2 fusion.26
  91.7 0.1 pad_maximum_fusion.2
  91.8 0.7 broadcast_in_dim.8
  92.4 6.7 %all-to-all-start.1 = ((f32[8,32,128]{2,1,0:T(8,128)}), f32[8,32,128]{2,1,0:T(8,128)S(1)}, u32[]{:S(2)}, u32[]{:S(2)}) async-start(f32[8,32,128]{2,1,0:T(8,128)} %broadcast_in_dim.8), calls=%async_computation.1 | async-start | bytes 262144 | tf_op jit(solution)/shard_map/all_to_all | solution.py:18
  99.1 0.1 pad.3.clone
  99.2 7.8 %all-to-all-done.1 = f32[8,32,128]{2,1,0:T(8,128)S(1)} async-done(((f32[8,32,128]{2,1,0:T(8,128)}), f32[8,32,128]{2,1,0:T(8,128)S(1)}, u32[]{:S(2)}, u32[]{:S(2)}) %all-to-all-start.1) | async-done | bytes 131104 | tf_op jit(solution)/shard_map/all_to_all | solution.py:18
  107.1 0.1 fusion.24
  107.2 0.3 convolution_bitcast_fusion
  107.5 17.0 %all_to_all.31 = f32[8,8,384]{2,1,0:T(8,128)S(1)} all-to-all(f32[8,8,384]{2,1,0:T(8,128)S(1)} %convolution_bitcast_fusion), channel_id=1, replica_groups=mesh['rep_x'=4,'rep_z'=12,'rep_core'=2,'shard'=8] {'rep_x','rep_core'}, dimensions={0} | all-to-all | bytes 196608 | tf_op jit(solution)/shard_map/all_to_all | solution.py:18
  124.6 15.1 %all_to_all.32 = f32[12,8,384]{2,1,0:T(8,128)S(1)} all-to-all(f32[12,8,384]{2,1,0:T(8,128)S(1)} %broadcast_in_dim.10), channel_id=1, replica_groups=mesh['rep_x'=4,'rep_z'=12,'rep_core'=2,'shard'=8] {'rep_z'}, dimensions={0} | all-to-all | bytes 294912 | tf_op jit(solution)/shard_map/all_to_all | solution.py:18
  139.7 0.7 broadcast_in_dim.11
  140.3 6.1 %all-to-all-start.4 = ((f32[8,8,384]{2,1,0:T(8,128)}), f32[8,8,384]{2,1,0:T(8,128)S(1)}, u32[]{:S(2)}, u32[]{:S(2)}) async-start(f32[8,8,384]{2,1,0:T(8,128)} %broadcast_in_dim.11), calls=%async_computation.4 | async-start | bytes 196608 | tf_op jit(solution)/shard_map/all_to_all | solution.py:18
  146.4 5.0 %all-to-all-done.4 = f32[8,8,384]{2,1,0:T(8,128)S(1)} async-done(((f32[8,8,384]{2,1,0:T(8,128)}), f32[8,8,384]{2,1,0:T(8,128)S(1)}, u32[]{:S(2)}, u32[]{:S(2)}) %all-to-all-start.4) | async-done | bytes 98336 | tf_op jit(solution)/shard_map/all_to_all | solution.py:18
  151.4 8.5 %shard_map.67 = (f32[64,64]{1,0:T(8,128)S(1)}, f32[64,256]{1,0:T(8,128)S(1)}, f32[8,8,128]{2,1,0:T(8,128)}) custom-call(f32[64,384]{1,0:T(8,128)S(1)} %bitcast.77, f32[64,64]{1,0:T(8,128)S(1)} %pad_maximum_fusion.1.left_ref), custom_call_target="tpu_custom_call" | custom-call | tf_op jit(solution)/shard_map/pallas_call | solution.py:180
  159.9 3.3 %all-to-all-start.5 = ((f32[8,8,128]{2,1,0:T(8,128)}), f32[8,8,128]{2,1,0:T(8,128)S(1)}, u32[]{:S(2)}, u32[]{:S(2)}) async-start(f32[8,8,128]{2,1,0:T(8,128)} %get-tuple-element.16), calls=%async_computation.5 | async-start | bytes 65536 | tf_op jit(solution)/shard_map/all_to_all | solution.py:18
  163.2 0.8 fusion
  164.0 6.0 %all-to-all-done.5.squares_ref = f32[8,8,128]{2,1,0:T(8,128)S(1)} async-done(((f32[8,8,128]{2,1,0:T(8,128)}), f32[8,8,128]{2,1,0:T(8,128)S(1)}, u32[]{:S(2)}, u32[]{:S(2)}) %all-to-all-start.5) | async-done | bytes 32800 | tf_op jit(solution)/shard_map/all_to_all | solution.py:18
  170.0 0.9 shard_map.68
  (10 shorter events, 0.1 us)
Async XLA Ops:
  0.6 0.9 copy-start
  5.7 3.0 %copy-start.1 = (f32[6144,256]{1,0:T(8,128)}, f32[6144,256]{1,0:T(8,128)S(1)}, u32[]{:S(2)}) copy-start(f32[6144,256]{1,0:T(8,128)S(1)} %fusion.25) | copy-start | bytes 18874372
  8.7 25.7 %collective-permute-start = (f32[3,4,3,64,256]{4,3,2,1,0:T(8,128)S(1)}, f32[3,4,3,64,256]{4,3,2,1,0:T(8,128)}, u32[]{:S(2)}, u32[]{:S(2)}) collective-permute-start(f32[3,4,3,64,256]{4,3,2,1,0:T(8,128)S(1)} %pad_maximum_fusion), channel_id=1, source_target_pairs={{0,8},{8,0},{1,9},{9,1},{2,10},{10,2},{3,11},{11,3},{4,12},{12,4},... | collective-permute-start | bytes 7077896 | tf_op jit(solution)/shard_map/ppermute | solution.py:28
  21.1 5.4 %collective-permute-start.1 = (f32[4,3,64,256]{3,2,1,0:T(8,128)}, f32[4,3,64,256]{3,2,1,0:T(8,128)}, u32[]{:S(2)}, u32[]{:S(2)}) collective-permute-start(f32[4,3,64,256]{3,2,1,0:T(8,128)} %get-tuple-element.24), channel_id=1, source_target_pairs={{0,8},{8,0},{1,9},{9,1},{2,10},{10,2},{3,11},{11,3},{4,12},{12,4},... | collective-permute-start | bytes 2359304 | tf_op jit(solution)/shard_map/ppermute | solution.py:28
  28.0 13.4 %collective-permute-start.2 = (f32[2,3,64,256]{3,2,1,0:T(8,128)S(1)}, f32[2,3,64,256]{3,2,1,0:T(8,128)S(1)}, u32[]{:S(2)}, u32[]{:S(2)}) collective-permute-start(f32[2,3,64,256]{3,2,1,0:T(8,128)S(1)} %get-tuple-element.23), channel_id=1, source_target_pairs={{0,192},{192,384},{384,576},{576,0},{1,193},{193,385},{385,577},{5... | collective-permute-start | bytes 1179656 | tf_op jit(solution)/shard_map/ppermute | solution.py:28
  29.9 13.5 %collective-permute-start.6 = (f32[2,3,64,256]{3,2,1,0:T(8,128)S(1)}, f32[2,3,64,256]{3,2,1,0:T(8,128)S(1)}, u32[]{:S(2)}, u32[]{:S(2)}) collective-permute-start(f32[2,3,64,256]{3,2,1,0:T(8,128)S(1)} %get-tuple-element.22), channel_id=1, source_target_pairs={{0,576},{192,0},{384,192},{576,384},{1,577},{193,1},{385,193},{577... | collective-permute-start | bytes 1179656 | tf_op jit(solution)/shard_map/ppermute | solution.py:28
  41.4 13.6 %collective-permute-start.3 = (f32[2,3,64,256]{3,2,1,0:T(8,128)S(1)}, f32[2,3,64,256]{3,2,1,0:T(8,128)S(1)}, u32[]{:S(2)}, u32[]{:S(2)}) collective-permute-start(f32[2,3,64,256]{3,2,1,0:T(8,128)S(1)} %add.203), channel_id=1, source_target_pairs={{0,192},{192,384},{384,576},{576,0},{1,193},{193,385},{385,577},{5... | collective-permute-start | bytes 1179656 | tf_op jit(solution)/shard_map/ppermute | solution.py:28
  43.4 48.0 %copy-start.2 = (f32[64,256]{1,0:T(8,128)S(1)}, f32[64,256]{1,0:T(8,128)}, u32[]{:S(2)}) copy-start(f32[64,256]{1,0:T(8,128)} %param.6) | copy-start | bytes 196612
  43.4 11.7 %collective-permute-start.7 = (f32[2,3,64,256]{3,2,1,0:T(8,128)S(1)}, f32[2,3,64,256]{3,2,1,0:T(8,128)S(1)}, u32[]{:S(2)}, u32[]{:S(2)}) collective-permute-start(f32[2,3,64,256]{3,2,1,0:T(8,128)S(1)} %add.208), channel_id=1, source_target_pairs={{0,576},{192,0},{384,192},{576,384},{1,577},{193,1},{385,193},{577... | collective-permute-start | bytes 1179656 | tf_op jit(solution)/shard_map/ppermute | solution.py:28
  48.1 15.4 %collective-permute-start.4 = (f32[2,3,64,256]{3,2,1,0:T(8,128)S(1)}, f32[2,3,64,256]{3,2,1,0:T(8,128)S(1)}, u32[]{:S(2)}, u32[]{:S(2)}) collective-permute-start(f32[2,3,64,256]{3,2,1,0:T(8,128)S(1)} %get-tuple-element.29), channel_id=1, source_target_pairs={{0,576},{192,0},{384,192},{576,384},{1,577},{193,1},{385,193},{577... | collective-permute-start | bytes 1179656 | tf_op jit(solution)/shard_map/ppermute | solution.py:28
  50.1 13.4 %collective-permute-start.5 = (f32[2,3,64,256]{3,2,1,0:T(8,128)S(1)}, f32[2,3,64,256]{3,2,1,0:T(8,128)S(1)}, u32[]{:S(2)}, u32[]{:S(2)}) collective-permute-start(f32[2,3,64,256]{3,2,1,0:T(8,128)S(1)} %get-tuple-element.21), channel_id=1, source_target_pairs={{0,192},{192,384},{384,576},{576,0},{1,193},{193,385},{385,577},{5... | collective-permute-start | bytes 1179656 | tf_op jit(solution)/shard_map/ppermute | solution.py:28
  53.5 37.9 %copy-start.3 = (f32[256,64]{0,1:T(8,128)S(1)}, f32[256,64]{0,1:T(8,128)}, u32[]{:S(2)}) copy-start(f32[256,64]{0,1:T(8,128)} %param.7) | copy-start | bytes 196612
  63.7 9.6 %collective-permute-start.8 = (f32[4,64,256]{2,1,0:T(8,128)S(1)}, f32[4,64,256]{2,1,0:T(8,128)S(1)}, u32[]{:S(2)}, u32[]{:S(2)}) collective-permute-start(f32[4,64,256]{2,1,0:T(8,128)S(1)} %get-tuple-element.30), channel_id=1, source_target_pairs={{0,16},{16,32},{32,48},{48,64},{64,80},{80,96},{96,112},{112,128},... | collective-permute-start | bytes 786440 | tf_op jit(solution)/shard_map/ppermute | solution.py:28
  65.7 8.6 %collective-permute-start.9 = (f32[4,64,256]{2,1,0:T(8,128)S(1)}, f32[4,64,256]{2,1,0:T(8,128)S(1)}, u32[]{:S(2)}, u32[]{:S(2)}) collective-permute-start(f32[4,64,256]{2,1,0:T(8,128)S(1)} %get-tuple-element.31), channel_id=1, source_target_pairs={{0,176},{16,0},{32,16},{48,32},{64,48},{80,64},{96,80},{112,96},{1... | collective-permute-start | bytes 786440 | tf_op jit(solution)/shard_map/ppermute | solution.py:28
  92.4 14.6 %all-to-all-start.1 = ((f32[8,32,128]{2,1,0:T(8,128)}), f32[8,32,128]{2,1,0:T(8,128)S(1)}, u32[]{:S(2)}, u32[]{:S(2)}) async-start(f32[8,32,128]{2,1,0:T(8,128)} %broadcast_in_dim.8), calls=%async_computation.1 | async-start | bytes 262144 | tf_op jit(solution)/shard_map/all_to_all | solution.py:18
  140.3 11.1 %all-to-all-start.4 = ((f32[8,8,384]{2,1,0:T(8,128)}), f32[8,8,384]{2,1,0:T(8,128)S(1)}, u32[]{:S(2)}, u32[]{:S(2)}) async-start(f32[8,8,384]{2,1,0:T(8,128)} %broadcast_in_dim.11), calls=%async_computation.4 | async-start | bytes 196608 | tf_op jit(solution)/shard_map/all_to_all | solution.py:18
  159.9 10.1 %all-to-all-start.5 = ((f32[8,8,128]{2,1,0:T(8,128)}), f32[8,8,128]{2,1,0:T(8,128)S(1)}, u32[]{:S(2)}, u32[]{:S(2)}) async-start(f32[8,8,128]{2,1,0:T(8,128)} %get-tuple-element.16), calls=%async_computation.5 | async-start | bytes 65536 | tf_op jit(solution)/shard_map/all_to_all | solution.py:18

commit v3 on v2

--- a/solution.py
+++ b/solution.py
@@ -38,7 +38,7 @@
     cols = inputs.shape[1]
     rows = cotangent.shape[1] // (nx * nz * 2)
     x, z, core = lax.axis_index(X), lax.axis_index(Z), lax.axis_index(CORE)
-    half = na // 2
+    half = na * nb * rows // 2
 
     partial = lax.dot_general(
         cotangent, inputs, (((0,), (0,)), ((), ())), preferred_element_type=jnp.float32
@@ -46,29 +46,32 @@
 
     def piece(ahead, which):
         at_x = lax.dynamic_index_in_dim(partial, (x + ahead) % nx, 0, keepdims=False)
-        return lax.dynamic_index_in_dim(at_x, which, 2, keepdims=False)
-
-    far = sent(piece(2, 1 - core), CORE, 1)
+        return lax.dynamic_index_in_dim(at_x, which, 2, keepdims=False).reshape(-1, cols)
+
     near = jnp.stack([piece(ahead, 1 - core) for ahead in (1, 3, 0)])
+    far, near, mine_far, mine_before, mine_after, mine = lax.optimization_barrier(
+        (piece(2, 1 - core), near, *(piece(ahead, core) for ahead in (2, 1, 3, 0)))
+    )
+    far = sent(far, CORE, 1)
     near = sent(near, CORE, 1)
-    mine = piece(2, core)
-    far_up, far_down = mine[:half] + far[:half], mine[half:] + far[half:]
+    far_up, far_down = mine_far[:half] + far[:half], mine_far[half:] + far[half:]
     relay_up = sent(far_up, X, 1)
     relay_down = sent(far_down, X, -1)
     near = gated(near, far_up, far_down)
-    before, after = piece(1, core), piece(3, core)
-    before_low, before_high = before[:half] + near[0, :half], before[half:] + near[0, half:]
-    after_low, after_high = after[:half] + near[1, :half], after[half:] + near[1, half:]
+    before_low = mine_before[:half] + near[0, :half]
+    before_high = mine_before[half:] + near[0, half:]
+    after_low = mine_after[:half] + near[1, :half]
+    after_high = mine_after[half:] + near[1, half:]
     high_below = sent(before_high, X, 1)
     low_above = sent(after_low, X, -1)
     relay_up = gated(relay_up, before_low, before_high, after_low)
     low_below = sent(before_low + relay_up, X, 1)
     relay_down = gated(relay_down, after_high, before_high, after_low)
     high_above = sent(after_high + relay_down, X, -1)
-    own = lax.optimization_barrier(piece(0, core) + near[2])
+    own = lax.optimization_barrier(mine + near[2])
     low = own[:half] + low_below + low_above
     high = own[half:] + high_below + high_above
-    over_x = jnp.concatenate([low, high], axis=0)
+    over_x = jnp.concatenate([low, high], axis=0).reshape(na, nb, rows, cols)
 
     kind = z % nb
 
@@ -104,23 +107,25 @@
     scaled = jnp.where(lane < rank, full * down * along, jnp.where(lane == row + rank, down, 0.0))
     blocks = [scaled[b * tile : (b + 1) * tile, :] for b in range(rank // tile)]
     row_of = lax.broadcasted_iota(jnp.int32, (tile, wide), 0)
+    full_tile = functools.partial(jnp.broadcast_to, shape=(tile, wide))
     for k in range(0, rank, 2):
         b, r = divmod(k, tile)
-        first, second = blocks[b][r : r + 1, :], blocks[b][r + 1 : r + 2, :]
-        a, c, d = first[:, k : k + 1], first[:, k + 1 : k + 2], second[:, k + 1 : k + 2]
+        first, second = full_tile(blocks[b][r : r + 1, :]), full_tile(blocks[b][r + 1 : r + 2, :])
+        a, c = full_tile(first[:, k : k + 1]), full_tile(first[:, k + 1 : k + 2])
+        d = full_tile(second[:, k + 1 : k + 2])
         det = a * d - c * c
         inv = 1.0 / det
-        to_first = (d * inv) * first - (c * inv) * second
-        to_second = (a * inv) * second - (c * inv) * first
-        unit_first = first * lax.rsqrt(a)
-        unit_second = (second - (c / a) * first) * lax.rsqrt(det / a)
+        to_first = (d * first - c * second) * inv
+        to_second = (a * second - c * first) * inv
         for i in range(b, rank // tile):
             old = blocks[i]
-            new = old - old[:, k : k + 1] * to_first - old[:, k + 1 : k + 2] * to_second
+            new = old - full_tile(old[:, k : k + 1]) * to_first
+            new = new - full_tile(old[:, k + 1 : k + 2]) * to_second
             if i == b:
+                root = lax.rsqrt(a)
                 new = jnp.where(row_of > r + 1, new, old)
-                new = jnp.where(row_of == r, unit_first, new)
-                new = jnp.where(row_of == r + 1, unit_second, new)
+                new = jnp.where(row_of == r, first * root, new)
+                new = jnp.where(row_of == r + 1, (a * second - c * first) * (root * lax.rsqrt(det)), new)
             blocks[i] = new
     inverse = jnp.concatenate(blocks, axis=0)[:, rank:]
     ortho_ref[...] = lax.dot_general(
@@ -140,7 +145,35 @@
         squares_ref[i] = squares
 
 
-def finish(ortho_ref, right_ref, squares_ref, factor_ref, update_ref, *, scale):
+def blend(pieces_ref, momentum_ref, right_ref, blended_ref, packed_ref):
+    blended = momentum_ref[...]
+    for i in range(pieces_ref.shape[0]):
+        blended = blended + pieces_ref[i]
+    blended_ref[...] = blended
+    left = lax.dot_general(
+        blended, right_ref[...], (((1,), (1,)), ((), ())), precision=HIGH,
+        preferred_element_type=jnp.float32,
+    )
+    half = left.shape[0] // 2
+    packed = jnp.concatenate([left[:half], left[half:]], axis=1)
+    for i in range(packed_ref.shape[0]):
+        packed_ref[i] = packed
+
+
+def project(packed_ref, blended_ref, left_ref, value_ref):
+    packed = packed_ref[0]
+    for i in range(1, packed_ref.shape[0]):
+        packed = packed + packed_ref[i]
+    rank = left_ref.shape[1]
+    left = jnp.concatenate([packed[:, :rank], packed[:, rank:]], axis=0)
+    left_ref[...] = left
+    both = jnp.concatenate([blended_ref[...], left, left], axis=1)
+    value_ref[...] = lax.dot_general(
+        left, both, (((0,), (0,)), ((), ())), precision=HIGH, preferred_element_type=jnp.float32
+    )
+
+
+def finish(ortho_ref, right_ref, squares_ref, blended_ref, momentum_ref, factor_ref, update_ref, *, scale):
     rank = ortho_ref.shape[1]
     squares = squares_ref[0]
     for i in range(1, squares_ref.shape[0]):
@@ -149,10 +182,13 @@
     row = lax.broadcasted_iota(jnp.int32, (rank, rank), 0)
     lane = lax.broadcasted_iota(jnp.int32, (rank, rank), 1)
     root = jnp.sum(jnp.where(row == lane, root, 0.0), axis=1, keepdims=True)
-    factor = right_ref[...] / root
+    right = right_ref[...]
+    factor = right / root
     factor_ref[...] = factor
-    update = jnp.dot(ortho_ref[...], factor, precision=HIGH, preferred_element_type=jnp.float32)
-    update_ref[...] = (scale * update).astype(update_ref.dtype)
+    ortho = ortho_ref[...]
+    dot = functools.partial(jnp.dot, precision=HIGH, preferred_element_type=jnp.float32)
+    momentum_ref[...] = blended_ref[...] - 0.05 * dot(ortho, right)
+    update_ref[...] = (scale * dot(ortho, factor)).astype(update_ref.dtype)
 
 
 def local_kernel(kernel, *out_shapes):
@@ -169,24 +205,22 @@
     in_total = momentum.shape[1] * shards
     rank = right_prev.shape[1]
     rows, cols = momentum.shape
-    blended = momentum + jnp.sum(gradient_rows(inputs, cotangent), axis=0)
-    left_part = jnp.dot(blended, right_prev, precision=HIGH)
-    packed = jnp.concatenate([left_part[: rows // 2], left_part[rows // 2 :]], axis=1)
-    packed = jnp.sum(from_everyone(packed, SHARD), axis=0)
-    left_raw = jnp.concatenate([packed[:, :rank], packed[:, rank:]], axis=0)
-    both = jnp.concatenate([blended, left_raw, jnp.zeros_like(left_raw)], axis=1)
-    total = rep_total(lax.dot_general(left_raw, both, (((0,), (0,)), ((), ())), precision=HIGH))
     f32 = functools.partial(jax.ShapeDtypeStruct, dtype=jnp.float32)
+    pieces = gradient_rows(inputs, cotangent)
+    blended, packed = local_kernel(
+        blend, f32((rows, cols)), f32((shards, rows // 2, 2 * rank))
+    )(pieces, momentum, right_prev.T)
+    left_raw, value = local_kernel(
+        project, f32((rows, rank)), f32((rank, cols + 2 * rank))
+    )(exchanged(packed, SHARD), blended)
     ortho, right_rows, squares = local_kernel(
         eliminate, f32((rows, rank)), f32((rank, cols)), f32((shards, 8, 2 * rank))
-    )(total, left_raw)
-    squares = exchanged(squares, SHARD)
-    new_momentum = blended - 0.05 * jnp.dot(ortho, right_rows, precision=HIGH)
+    )(rep_total(value), left_raw)
     scale = (out_total * in_total / rank) ** 0.5
-    factor_rows, update = local_kernel(
+    new_momentum, factor_rows, update = local_kernel(
         functools.partial(finish, scale=scale),
-        f32((rank, cols)), jax.ShapeDtypeStruct((rows, cols), jnp.bfloat16),
-    )(ortho, right_rows, squares)
+        f32((rows, cols)), f32((rank, cols)), jax.ShapeDtypeStruct((rows, cols), jnp.bfloat16),
+    )(ortho, right_rows, exchanged(squares, SHARD), blended)
     return (new_momentum, factor_rows.T, update)
 
 

time: 172 us -> 166 us (0.965)
  blocking collectives: 49.2 us -> 80.8 us
  starting transfers between devices: 56.1 us -> 40.6 us
  waiting for transfers between devices: 38.9 us -> 24.9 us
  local copies, waits for them, and re-layouts: 5.16 us -> 1.73 us
  Pallas kernels: 9.4 us -> 6.73 us
    all_to_all x3 -> x6, blocking collectives: 49.2 us -> 80.8 us  [exchanged(): lax.all_to_all(pieces, axis, 0, 0, tiled=True, axis_index_groups=groups)]
    all_to_all x3 -> x0, waiting for transfers between devices: 18.8 us -> none  [exchanged(): lax.all_to_all(pieces, axis, 0, 0, tiled=True, axis_index_groups=groups)]
    all_to_all x3 -> x0, starting transfers between devices: 16.1 us -> none  [exchanged(): lax.all_to_all(pieces, axis, 0, 0, tiled=True, axis_index_groups=groups)]
    ppermute x10, waiting for transfers between devices: 20.1 us -> 24.9 us  [sent(): lax.ppermute(value, axis, [(i, (i + distance) % size) for i in range(size)])]
    pallas_call x1, Pallas kernels: 8.49 us -> 5.16 us  [body(): local_kernel(eliminate, f32((rows, rank)), f32((rank, cols)), f32((shards...]
    add x5 -> x4, other arithmetic: 5.09 us -> 2.93 us  [the longest x1 1.5 us: gradient_rows(): low = own[:half] + low_below + low_above]
  transfers between devices with their start and end apart: 13 -> 10, of which waited for: 8 -> 7; matrix products, arithmetic and copies ran while one was open for 3% -> 2% of each run, Pallas kernels for 0% -> 0%
where the time goes in v3:
time: 166 us; the launch traced here: 165 us
  blocking collectives  80.8 us (49%)
  starting transfers between devices  40.6 us (24%)
  waiting for transfers between devices  24.9 us (15%)
  Pallas kernels  6.73 us (4%)
  other arithmetic  4.84 us (3%)
  matrix products  4.17 us (3%)
  local copies, waits for them, and re-layouts  1.73 us (1%)
    all_to_all x6, blocking collectives, exchanged(): lax.all_to_all(pieces, axis, 0, 0, tiled=True, axis_index_groups=groups)  80.8 us
    ppermute x10, starting transfers between devices, sent(): lax.ppermute(value, axis, [(i, (i + distance) % size) for i in range(size)])  40.6 us
    ppermute x10, waiting for transfers between devices, sent(): lax.ppermute(value, axis, [(i, (i + distance) % size) for i in range(size)])  24.9 us
    pallas_call x1, Pallas kernels, body(): local_kernel(eliminate, f32((rows, rank)), f32((rank, cols)), f32((shards...  5.16 us
    dot_general x1, matrix products, gradient_rows(): lax.dot_general(cotangent, inputs, (((0,), (0,)), ((), ())), preferred_el...  4.17 us
  transfers between devices with their start and end apart: 10, of which 7 were waited for; matrix products, arithmetic and copies ran while one was open for 2% of the time, Pallas kernels for 0%

profile of v3, /device:TPU:1, one launch (start us, length us, event | category | flops | bytes accessed | tf_op | source)
XLA Modules:
  0.0 164.8 jit_solution(11961372618713455571)
XLA Ops:
  0.6 0.0 copy-start
  0.7 0.8 copy-done
  1.6 4.2 %fusion.3 = f32[6144,256]{1,0:T(8,128)S(1)} fusion(bf16[384,6144]{1,0:T(8,128)(2,1)} %param.5, bf16[384,256]{1,0:T(8,128)(2,1)S(1)} %copy-done), kind=kOutput, calls=%fused_computation.25 | convolution fusion | flops 1207959552 | bytes 11206656 | tf_op jit(solution)/shard_map/dot_general | solution.py:43
  5.7 0.8 constant_dynamic-slice_fusion
  6.6 0.2 pad_maximum_fusion
  6.7 12.4 %collective-permute-start = (f32[3,768,256]{2,1,0:T(8,128)S(1)}, f32[3,768,256]{2,1,0:T(8,128)S(1)}, u32[]{:S(2)}, u32[]{:S(2)}) collective-permute-start(f32[3,768,256]{2,1,0:T(8,128)S(1)} %pad_maximum_fusion), channel_id=1, source_target_pairs={{0,8},{8,0},{1,9},{9,1},{2,10},{10,2},{3,11},{11,3},{4,12},{12,4},... | collective-permute-start | bytes 7077896 | tf_op jit(solution)/shard_map/ppermute | solution.py:28
  19.1 1.9 %collective-permute-start.1 = (f32[768,256]{1,0:T(8,128)S(1)}, f32[768,256]{1,0:T(8,128)S(1)}, u32[]{:S(2)}, u32[]{:S(2)}) collective-permute-start(f32[768,256]{1,0:T(8,128)S(1)} %bitcast.47), channel_id=1, source_target_pairs={{0,8},{8,0},{1,9},{9,1},{2,10},{10,2},{3,11},{11,3},{4,12},{12,4},... | collective-permute-start | bytes 2359304 | tf_op jit(solution)/shard_map/ppermute | solution.py:28
  21.0 3.3 %collective-permute-done.1 = f32[768,256]{1,0:T(8,128)S(1)} collective-permute-done((f32[768,256]{1,0:T(8,128)S(1)}, f32[768,256]{1,0:T(8,128)S(1)}, u32[]{:S(2)}, u32[]{:S(2)}) %collective-permute-start.1) | collective-permute-done | bytes 786464 | tf_op jit(solution)/shard_map/ppermute | solution.py:28
  24.4 0.1 slice_add_fusion.2
  24.5 1.9 %collective-permute-start.6 = (f32[384,256]{1,0:T(8,128)S(1)}, f32[384,256]{1,0:T(8,128)S(1)}, u32[]{:S(2)}, u32[]{:S(2)}) collective-permute-start(f32[384,256]{1,0:T(8,128)S(1)} %get-tuple-element.55), channel_id=1, source_target_pairs={{0,576},{192,0},{384,192},{576,384},{1,577},{193,1},{385,193},{577... | collective-permute-start | bytes 1179656 | tf_op jit(solution)/shard_map/ppermute | solution.py:28
  26.4 3.4 %collective-permute-start.2 = (f32[384,256]{1,0:T(8,128)S(1)}, f32[384,256]{1,0:T(8,128)S(1)}, u32[]{:S(2)}, u32[]{:S(2)}) collective-permute-start(f32[384,256]{1,0:T(8,128)S(1)} %get-tuple-element.56), channel_id=1, source_target_pairs={{0,192},{192,384},{384,576},{576,0},{1,193},{193,385},{385,577},{5... | collective-permute-start | bytes 1179656 | tf_op jit(solution)/shard_map/ppermute | solution.py:28
  29.8 0.0 collective-permute-done
  29.8 1.2 bitcast_add_fusion.4
  31.0 5.7 %collective-permute-done.6 = f32[384,256]{1,0:T(8,128)S(1)} collective-permute-done((f32[384,256]{1,0:T(8,128)S(1)}, f32[384,256]{1,0:T(8,128)S(1)}, u32[]{:S(2)}, u32[]{:S(2)}) %collective-permute-start.6) | collective-permute-done | bytes 393248 | tf_op jit(solution)/shard_map/ppermute | solution.py:28
  36.7 0.8 add.205
  37.5 3.4 %collective-permute-start.7 = (f32[384,256]{1,0:T(8,128)}, f32[384,256]{1,0:T(8,128)}, u32[]{:S(2)}, u32[]{:S(2)}) collective-permute-start(f32[384,256]{1,0:T(8,128)} %add.205), channel_id=1, source_target_pairs={{0,576},{192,0},{384,192},{576,384},{1,577},{193,1},{385,193},{577... | collective-permute-start | bytes 1179656 | tf_op jit(solution)/shard_map/ppermute | solution.py:28
  40.9 0.0 collective-permute-done.2
  40.9 0.8 add.200
  41.7 1.9 %collective-permute-start.3 = (f32[384,256]{1,0:T(8,128)}, f32[384,256]{1,0:T(8,128)}, u32[]{:S(2)}, u32[]{:S(2)}) collective-permute-start(f32[384,256]{1,0:T(8,128)} %add.200), channel_id=1, source_target_pairs={{0,192},{192,384},{384,576},{576,0},{1,193},{193,385},{385,577},{5... | collective-permute-start | bytes 1179656 | tf_op jit(solution)/shard_map/ppermute | solution.py:28
  43.6 4.6 %collective-permute-start.4 = (f32[384,256]{1,0:T(8,128)}, f32[384,256]{1,0:T(8,128)}, u32[]{:S(2)}, u32[]{:S(2)}) collective-permute-start(f32[384,256]{1,0:T(8,128)} %get-tuple-element.54), channel_id=1, source_target_pairs={{0,576},{192,0},{384,192},{576,384},{1,577},{193,1},{385,193},{577... | collective-permute-start | bytes 1179656 | tf_op jit(solution)/shard_map/ppermute | solution.py:28
  48.2 1.9 %collective-permute-start.5 = (f32[384,256]{1,0:T(8,128)}, f32[384,256]{1,0:T(8,128)}, u32[]{:S(2)}, u32[]{:S(2)}) collective-permute-start(f32[384,256]{1,0:T(8,128)} %get-tuple-element.50), channel_id=1, source_target_pairs={{0,192},{192,384},{384,576},{576,0},{1,193},{193,385},{385,577},{5... | collective-permute-start | bytes 1179656 | tf_op jit(solution)/shard_map/ppermute | solution.py:28
  50.2 0.1 bitcast_add_fusion
  50.3 0.0 collective-permute-done.7
  50.3 4.2 %collective-permute-done.3 = f32[384,256]{1,0:T(8,128)} collective-permute-done((f32[384,256]{1,0:T(8,128)}, f32[384,256]{1,0:T(8,128)}, u32[]{:S(2)}, u32[]{:S(2)}) %collective-permute-start.3) | collective-permute-done | bytes 393248 | tf_op jit(solution)/shard_map/ppermute | solution.py:28
  54.6 3.0 %collective-permute-done.4 = f32[384,256]{1,0:T(8,128)} collective-permute-done((f32[384,256]{1,0:T(8,128)}, f32[384,256]{1,0:T(8,128)}, u32[]{:S(2)}, u32[]{:S(2)}) %collective-permute-start.4) | collective-permute-done | bytes 393248 | tf_op jit(solution)/shard_map/ppermute | solution.py:28
  57.5 5.5 %collective-permute-done.5 = f32[384,256]{1,0:T(8,128)} collective-permute-done((f32[384,256]{1,0:T(8,128)}, f32[384,256]{1,0:T(8,128)}, u32[]{:S(2)}, u32[]{:S(2)}) %collective-permute-start.5) | collective-permute-done | bytes 393248 | tf_op jit(solution)/shard_map/ppermute | solution.py:28
  63.0 1.5 fusion.1
  64.5 0.0 copy-start.1
  64.5 0.0 copy-start.2
  64.5 0.1 pad_maximum_fusion.1
  64.6 1.9 %collective-permute-start.8 = (f32[4,64,256]{2,1,0:T(8,128)S(1)}, f32[4,64,256]{2,1,0:T(8,128)S(1)}, u32[]{:S(2)}, u32[]{:S(2)}) collective-permute-start(f32[4,64,256]{2,1,0:T(8,128)S(1)} %get-tuple-element.57), channel_id=1, source_target_pairs={{0,16},{16,32},{32,48},{48,64},{64,80},{80,96},{96,112},{112,128},... | collective-permute-start | bytes 786440 | tf_op jit(solution)/shard_map/ppermute | solution.py:28
  66.6 7.3 %collective-permute-start.9 = (f32[4,64,256]{2,1,0:T(8,128)S(1)}, f32[4,64,256]{2,1,0:T(8,128)S(1)}, u32[]{:S(2)}, u32[]{:S(2)}) collective-permute-start(f32[4,64,256]{2,1,0:T(8,128)S(1)} %get-tuple-element.58), channel_id=1, source_target_pairs={{0,176},{16,0},{32,16},{48,32},{64,48},{80,64},{96,80},{112,96},{1... | collective-permute-start | bytes 786440 | tf_op jit(solution)/shard_map/ppermute | solution.py:28
  73.9 2.4 %collective-permute-done.8 = f32[4,64,256]{2,1,0:T(8,128)S(1)} collective-permute-done((f32[4,64,256]{2,1,0:T(8,128)S(1)}, f32[4,64,256]{2,1,0:T(8,128)S(1)}, u32[]{:S(2)}, u32[]{:S(2)}) %collective-permute-start.8) | collective-permute-done | bytes 262176 | tf_op jit(solution)/shard_map/ppermute | solution.py:28
  76.3 0.9 collective-permute-done.9
  77.1 0.1 fusion.2
  77.2 17.2 %all_to_all.30.pieces_ref = f32[4,64,256]{2,1,0:T(8,128)S(1)} all-to-all(f32[4,64,256]{2,1,0:T(8,128)S(1)} %fusion.2), channel_id=1, replica_groups={{0,48,96,144},{16,64,112,160},{32,80,128,176},{1,49,97,145},{17,65,113,..., dimensions={0} | all-to-all | bytes 524288 | tf_op jit(solution)/shard_map/all_to_all | solution.py:18
  94.4 0.0 copy-done.1
  94.4 0.0 copy-done.2
  94.4 0.3 shard_map.67
  94.7 14.5 %all_to_all.31.packed_ref = f32[8,32,128]{2,1,0:T(8,128)S(1)} all-to-all(f32[8,32,128]{2,1,0:T(8,128)S(1)} %get-tuple-element.31), channel_id=1, replica_groups=mesh['rep_x'=4,'rep_z'=12,'rep_core'=2,'shard'=8] {'shard'}, dimensions={0} | all-to-all | bytes 262144 | tf_op jit(solution)/shard_map/all_to_all | solution.py:18
  109.2 0.4 shard_map.68
  109.6 14.5 %all_to_all.32 = f32[8,8,384]{2,1,0:T(8,128)S(1)} all-to-all(f32[8,8,384]{2,1,0:T(8,128)S(1)} %bitcast.35), channel_id=1, replica_groups=mesh['rep_x'=4,'rep_z'=12,'rep_core'=2,'shard'=8] {'rep_x','rep_core'}, dimensions={0} | all-to-all | bytes 196608 | tf_op jit(solution)/shard_map/all_to_all | solution.py:18
  124.1 15.1 %all_to_all.33 = f32[12,8,384]{2,1,0:T(8,128)S(1)} all-to-all(f32[12,8,384]{2,1,0:T(8,128)S(1)} %broadcast_in_dim.4), channel_id=1, replica_groups=mesh['rep_x'=4,'rep_z'=12,'rep_core'=2,'shard'=8] {'rep_z'}, dimensions={0} | all-to-all | bytes 294912 | tf_op jit(solution)/shard_map/all_to_all | solution.py:18
  139.3 10.2 %all_to_all.34 = f32[8,8,384]{2,1,0:T(8,128)S(1)} all-to-all(f32[8,8,384]{2,1,0:T(8,128)S(1)} %broadcast_in_dim.5), channel_id=1, replica_groups=mesh['rep_x'=4,'rep_z'=12,'rep_core'=2,'shard'=8] {'rep_x','rep_core'}, dimensions={0} | all-to-all | bytes 196608 | tf_op jit(solution)/shard_map/all_to_all | solution.py:18
  149.4 5.2 %shard_map.69 = (f32[64,64]{1,0:T(8,128)S(1)}, f32[64,256]{1,0:T(8,128)S(1)}, f32[8,8,128]{2,1,0:T(8,128)S(1)}) custom-call(f32[64,384]{1,0:T(8,128)S(1)} %bitcast.34, f32[64,64]{1,0:T(8,128)S(1)} %get-tuple-element.34.left_ref), custom_call_target="tpu_custom_call" | custom-call | tf_op jit(solution)/shard_map/pallas_call | solution.py:216
  154.6 9.3 %all_to_all.35.squares_ref = f32[8,8,128]{2,1,0:T(8,128)S(1)} all-to-all(f32[8,8,128]{2,1,0:T(8,128)S(1)} %get-tuple-element.37), channel_id=1, replica_groups=mesh['rep_x'=4,'rep_z'=12,'rep_core'=2,'shard'=8] {'shard'}, dimensions={0} | all-to-all | bytes 65536 | tf_op jit(solution)/shard_map/all_to_all | solution.py:18
  163.9 0.9 shard_map.70
  (5 shorter events, 0.1 us)
Async XLA Ops:
  0.6 0.9 copy-start
  6.7 23.1 %collective-permute-start = (f32[3,768,256]{2,1,0:T(8,128)S(1)}, f32[3,768,256]{2,1,0:T(8,128)S(1)}, u32[]{:S(2)}, u32[]{:S(2)}) collective-permute-start(f32[3,768,256]{2,1,0:T(8,128)S(1)} %pad_maximum_fusion), channel_id=1, source_target_pairs={{0,8},{8,0},{1,9},{9,1},{2,10},{10,2},{3,11},{11,3},{4,12},{12,4},... | collective-permute-start | bytes 7077896 | tf_op jit(solution)/shard_map/ppermute | solution.py:28
  19.1 5.3 %collective-permute-start.1 = (f32[768,256]{1,0:T(8,128)S(1)}, f32[768,256]{1,0:T(8,128)S(1)}, u32[]{:S(2)}, u32[]{:S(2)}) collective-permute-start(f32[768,256]{1,0:T(8,128)S(1)} %bitcast.47), channel_id=1, source_target_pairs={{0,8},{8,0},{1,9},{9,1},{2,10},{10,2},{3,11},{11,3},{4,12},{12,4},... | collective-permute-start | bytes 2359304 | tf_op jit(solution)/shard_map/ppermute | solution.py:28
  24.5 12.2 %collective-permute-start.6 = (f32[384,256]{1,0:T(8,128)S(1)}, f32[384,256]{1,0:T(8,128)S(1)}, u32[]{:S(2)}, u32[]{:S(2)}) collective-permute-start(f32[384,256]{1,0:T(8,128)S(1)} %get-tuple-element.55), channel_id=1, source_target_pairs={{0,576},{192,0},{384,192},{576,384},{1,577},{193,1},{385,193},{577... | collective-permute-start | bytes 1179656 | tf_op jit(solution)/shard_map/ppermute | solution.py:28
  26.4 14.5 %collective-permute-start.2 = (f32[384,256]{1,0:T(8,128)S(1)}, f32[384,256]{1,0:T(8,128)S(1)}, u32[]{:S(2)}, u32[]{:S(2)}) collective-permute-start(f32[384,256]{1,0:T(8,128)S(1)} %get-tuple-element.56), channel_id=1, source_target_pairs={{0,192},{192,384},{384,576},{576,0},{1,193},{193,385},{385,577},{5... | collective-permute-start | bytes 1179656 | tf_op jit(solution)/shard_map/ppermute | solution.py:28
  37.5 12.8 %collective-permute-start.7 = (f32[384,256]{1,0:T(8,128)}, f32[384,256]{1,0:T(8,128)}, u32[]{:S(2)}, u32[]{:S(2)}) collective-permute-start(f32[384,256]{1,0:T(8,128)} %add.205), channel_id=1, source_target_pairs={{0,576},{192,0},{384,192},{576,384},{1,577},{193,1},{385,193},{577... | collective-permute-start | bytes 1179656 | tf_op jit(solution)/shard_map/ppermute | solution.py:28
  41.7 12.9 %collective-permute-start.3 = (f32[384,256]{1,0:T(8,128)}, f32[384,256]{1,0:T(8,128)}, u32[]{:S(2)}, u32[]{:S(2)}) collective-permute-start(f32[384,256]{1,0:T(8,128)} %add.200), channel_id=1, source_target_pairs={{0,192},{192,384},{384,576},{576,0},{1,193},{193,385},{385,577},{5... | collective-permute-start | bytes 1179656 | tf_op jit(solution)/shard_map/ppermute | solution.py:28
  43.6 13.9 %collective-permute-start.4 = (f32[384,256]{1,0:T(8,128)}, f32[384,256]{1,0:T(8,128)}, u32[]{:S(2)}, u32[]{:S(2)}) collective-permute-start(f32[384,256]{1,0:T(8,128)} %get-tuple-element.54), channel_id=1, source_target_pairs={{0,576},{192,0},{384,192},{576,384},{1,577},{193,1},{385,193},{577... | collective-permute-start | bytes 1179656 | tf_op jit(solution)/shard_map/ppermute | solution.py:28
  48.2 14.8 %collective-permute-start.5 = (f32[384,256]{1,0:T(8,128)}, f32[384,256]{1,0:T(8,128)}, u32[]{:S(2)}, u32[]{:S(2)}) collective-permute-start(f32[384,256]{1,0:T(8,128)} %get-tuple-element.50), channel_id=1, source_target_pairs={{0,192},{192,384},{384,576},{576,0},{1,193},{193,385},{385,577},{5... | collective-permute-start | bytes 1179656 | tf_op jit(solution)/shard_map/ppermute | solution.py:28
  64.5 29.9 %copy-start.1 = (f32[64,256]{1,0:T(8,128)S(1)}, f32[64,256]{1,0:T(8,128)}, u32[]{:S(2)}) copy-start(f32[64,256]{1,0:T(8,128)} %momentum_ref.1) | copy-start | bytes 196612
  64.5 29.9 %copy-start.2 = (f32[256,64]{0,1:T(8,128)S(1)}, f32[256,64]{0,1:T(8,128)}, u32[]{:S(2)}) copy-start(f32[256,64]{0,1:T(8,128)} %param.7) | copy-start | bytes 196612
  64.6 11.6 %collective-permute-start.8 = (f32[4,64,256]{2,1,0:T(8,128)S(1)}, f32[4,64,256]{2,1,0:T(8,128)S(1)}, u32[]{:S(2)}, u32[]{:S(2)}) collective-permute-start(f32[4,64,256]{2,1,0:T(8,128)S(1)} %get-tuple-element.57), channel_id=1, source_target_pairs={{0,16},{16,32},{32,48},{48,64},{64,80},{80,96},{96,112},{112,128},... | collective-permute-start | bytes 786440 | tf_op jit(solution)/shard_map/ppermute | solution.py:28
  66.6 10.6 %collective-permute-start.9 = (f32[4,64,256]{2,1,0:T(8,128)S(1)}, f32[4,64,256]{2,1,0:T(8,128)S(1)}, u32[]{:S(2)}, u32[]{:S(2)}) collective-permute-start(f32[4,64,256]{2,1,0:T(8,128)S(1)} %get-tuple-element.58), channel_id=1, source_target_pairs={{0,176},{16,0},{32,16},{48,32},{64,48},{80,64},{96,80},{112,96},{1... | collective-permute-start | bytes 786440 | tf_op jit(solution)/shard_map/ppermute | solution.py:28

commit v4 on v3

--- a/solution.py
+++ b/solution.py
@@ -38,7 +38,7 @@
     cols = inputs.shape[1]
     rows = cotangent.shape[1] // (nx * nz * 2)
     x, z, core = lax.axis_index(X), lax.axis_index(Z), lax.axis_index(CORE)
-    half = na * nb * rows // 2
+    half = na * nb * rows * 7 // 12 // 8 * 8
 
     partial = lax.dot_general(
         cotangent, inputs, (((0,), (0,)), ((), ())), preferred_element_type=jnp.float32
@@ -58,19 +58,22 @@
     relay_up = sent(far_up, X, 1)
     relay_down = sent(far_down, X, -1)
     near = gated(near, far_up, far_down)
-    before_low = mine_before[:half] + near[0, :half]
     before_high = mine_before[half:] + near[0, half:]
     after_low = mine_after[:half] + near[1, :half]
-    after_high = mine_after[half:] + near[1, half:]
     high_below = sent(before_high, X, 1)
     low_above = sent(after_low, X, -1)
-    relay_up = gated(relay_up, before_low, before_high, after_low)
-    low_below = sent(before_low + relay_up, X, 1)
-    relay_down = gated(relay_down, after_high, before_high, after_low)
-    high_above = sent(after_high + relay_down, X, -1)
-    own = lax.optimization_barrier(mine + near[2])
-    low = own[:half] + low_below + low_above
-    high = own[half:] + high_below + high_above
+    near = gated(near, before_high, after_low)
+    own_low = lax.optimization_barrier(mine[:half] + near[2, :half])
+    near = gated(near, own_low)
+    before_low = lax.optimization_barrier(mine_before[:half] + near[0, :half] + relay_up)
+    low_below = sent(before_low, X, 1)
+    near = gated(near, before_low)
+    own_high = lax.optimization_barrier(mine[half:] + near[2, half:])
+    near = gated(near, own_high)
+    after_high = lax.optimization_barrier(mine_after[half:] + near[1, half:] + relay_down)
+    high_above = sent(after_high, X, -1)
+    low = own_low + low_below + low_above
+    high = own_high + high_below + high_above
     over_x = jnp.concatenate([low, high], axis=0).reshape(na, nb, rows, cols)
 
     kind = z % nb

time: 166 us -> 163 us (0.982)
  other arithmetic: 4.84 us -> 2.63 us
    add x5 -> x9, other arithmetic: 4.45 us -> 2.3 us  [the longest x1 1.03 us: gradient_rows(): high = own_high + high_below + high_above]
  transfers between devices with their start and end apart: 10 -> 10, of which waited for: 7 -> 6; matrix products, arithmetic and copies ran while one was open for 2% -> 1% of each run, Pallas kernels for 0% -> 0%
where the time goes in v4:
time: 163 us; the launch traced here: 162 us
  blocking collectives  81 us (50%)
  starting transfers between devices  39.8 us (24%)
  waiting for transfers between devices  25 us (15%)
  Pallas kernels  6.72 us (4%)
  matrix products  4.17 us (3%)
  other arithmetic  2.63 us (2%)
  local copies, waits for them, and re-layouts  1.74 us (1%)
    all_to_all x6, blocking collectives, exchanged(): lax.all_to_all(pieces, axis, 0, 0, tiled=True, axis_index_groups=groups)  81 us
    ppermute x10, starting transfers between devices, sent(): lax.ppermute(value, axis, [(i, (i + distance) % size) for i in range(size)])  39.8 us
    ppermute x10, waiting for transfers between devices, sent(): lax.ppermute(value, axis, [(i, (i + distance) % size) for i in range(size)])  25 us
    pallas_call x1, Pallas kernels, body(): local_kernel(eliminate, f32((rows, rank)), f32((rank, cols)), f32((shards...  5.16 us
    dot_general x1, matrix products, gradient_rows(): lax.dot_general(cotangent, inputs, (((0,), (0,)), ((), ())), preferred_el...  4.17 us
  transfers between devices with their start and end apart: 10, of which 6 were waited for; matrix products, arithmetic and copies ran while one was open for 1% of the time, Pallas kernels for 0%

profile of v4, /device:TPU:1, one launch (start us, length us, event | category | flops | bytes accessed | tf_op | source)
XLA Modules:
  0.0 162.1 jit_solution(15224226550713675838)
XLA Ops:
  0.6 0.0 copy-start
  0.7 0.8 copy-done
  1.6 4.2 %fusion.3 = f32[6144,256]{1,0:T(8,128)S(1)} fusion(bf16[384,6144]{1,0:T(8,128)(2,1)} %param.5, bf16[384,256]{1,0:T(8,128)(2,1)S(1)} %copy-done), kind=kOutput, calls=%fused_computation.26 | convolution fusion | flops 1207959552 | bytes 11206656 | tf_op jit(solution)/shard_map/dot_general | solution.py:43
  5.7 0.8 constant_dynamic-slice_fusion
  6.6 0.2 pad_maximum_fusion
  6.7 12.4 %collective-permute-start = (f32[3,768,256]{2,1,0:T(8,128)S(1)}, f32[3,768,256]{2,1,0:T(8,128)S(1)}, u32[]{:S(2)}, u32[]{:S(2)}) collective-permute-start(f32[3,768,256]{2,1,0:T(8,128)S(1)} %pad_maximum_fusion), channel_id=1, source_target_pairs={{0,8},{8,0},{1,9},{9,1},{2,10},{10,2},{3,11},{11,3},{4,12},{12,4},... | collective-permute-start | bytes 7077896 | tf_op jit(solution)/shard_map/ppermute | solution.py:28
  19.1 1.9 %collective-permute-start.1 = (f32[768,256]{1,0:T(8,128)S(1)}, f32[768,256]{1,0:T(8,128)S(1)}, u32[]{:S(2)}, u32[]{:S(2)}) collective-permute-start(f32[768,256]{1,0:T(8,128)S(1)} %bitcast.57), channel_id=1, source_target_pairs={{0,8},{8,0},{1,9},{9,1},{2,10},{10,2},{3,11},{11,3},{4,12},{12,4},... | collective-permute-start | bytes 2359304 | tf_op jit(solution)/shard_map/ppermute | solution.py:28
  21.0 3.3 %collective-permute-done.1 = f32[768,256]{1,0:T(8,128)S(1)} collective-permute-done((f32[768,256]{1,0:T(8,128)S(1)}, f32[768,256]{1,0:T(8,128)S(1)}, u32[]{:S(2)}, u32[]{:S(2)}) %collective-permute-start.1) | collective-permute-done | bytes 786464 | tf_op jit(solution)/shard_map/ppermute | solution.py:28
  24.4 0.1 slice_add_fusion
  24.4 1.9 %collective-permute-start.2 = (f32[448,256]{1,0:T(8,128)S(1)}, f32[448,256]{1,0:T(8,128)S(1)}, u32[]{:S(2)}, u32[]{:S(2)}) collective-permute-start(f32[448,256]{1,0:T(8,128)S(1)} %slice_add_fusion), channel_id=1, source_target_pairs={{0,192},{192,384},{384,576},{576,0},{1,193},{193,385},{385,577},{5... | collective-permute-start | bytes 1376264 | tf_op jit(solution)/shard_map/ppermute | solution.py:28
  26.4 4.6 %collective-permute-start.6 = (f32[320,256]{1,0:T(8,128)S(1)}, f32[320,256]{1,0:T(8,128)S(1)}, u32[]{:S(2)}, u32[]{:S(2)}) collective-permute-start(f32[320,256]{1,0:T(8,128)S(1)} %slice_add_fusion.1), channel_id=1, source_target_pairs={{0,576},{192,0},{384,192},{576,384},{1,577},{193,1},{385,193},{577... | collective-permute-start | bytes 983048 | tf_op jit(solution)/shard_map/ppermute | solution.py:28
  31.0 0.0 collective-permute-done
  31.0 0.1 bitcast_add_fusion.2
  31.1 0.8 bitcast_add_fusion.5
  31.8 0.1 bitcast_add_fusion.1
  31.9 7.4 %collective-permute-done.2 = f32[448,256]{1,0:T(8,128)S(1)} collective-permute-done((f32[448,256]{1,0:T(8,128)S(1)}, f32[448,256]{1,0:T(8,128)S(1)}, u32[]{:S(2)}, u32[]{:S(2)}) %collective-permute-start.2) | collective-permute-done | bytes 458784 | tf_op jit(solution)/shard_map/ppermute | solution.py:28
  39.3 0.1 fusion
  39.4 0.0 collective-permute-done.6
  39.4 0.1 fusion.1
  39.5 3.3 %collective-permute-start.7 = (f32[320,256]{1,0:T(8,128)S(1)}, f32[320,256]{1,0:T(8,128)S(1)}, u32[]{:S(2)}, u32[]{:S(2)}) collective-permute-start(f32[320,256]{1,0:T(8,128)S(1)} %fusion.1), channel_id=1, source_target_pairs={{0,576},{192,0},{384,192},{576,384},{1,577},{193,1},{385,193},{577... | collective-permute-start | bytes 983048 | tf_op jit(solution)/shard_map/ppermute | solution.py:28
  42.8 2.0 %collective-permute-start.5 = (f32[320,256]{1,0:T(8,128)}, f32[320,256]{1,0:T(8,128)}, u32[]{:S(2)}, u32[]{:S(2)}) collective-permute-start(f32[320,256]{1,0:T(8,128)} %bitcast_add_fusion.5), channel_id=1, source_target_pairs={{0,192},{192,384},{384,576},{576,0},{1,193},{193,385},{385,577},{5... | collective-permute-start | bytes 983048 | tf_op jit(solution)/shard_map/ppermute | solution.py:28
  44.8 1.9 %collective-permute-start.3 = (f32[448,256]{1,0:T(8,128)S(1)}, f32[448,256]{1,0:T(8,128)S(1)}, u32[]{:S(2)}, u32[]{:S(2)}) collective-permute-start(f32[448,256]{1,0:T(8,128)S(1)} %fusion), channel_id=1, source_target_pairs={{0,192},{192,384},{384,576},{576,0},{1,193},{193,385},{385,577},{5... | collective-permute-start | bytes 1376264 | tf_op jit(solution)/shard_map/ppermute | solution.py:28
  46.7 4.6 %collective-permute-start.4 = (f32[448,256]{1,0:T(8,128)S(1)}, f32[448,256]{1,0:T(8,128)S(1)}, u32[]{:S(2)}, u32[]{:S(2)}) collective-permute-start(f32[448,256]{1,0:T(8,128)S(1)} %bitcast_add_fusion.2), channel_id=1, source_target_pairs={{0,576},{192,0},{384,192},{576,384},{1,577},{193,1},{385,193},{577... | collective-permute-start | bytes 1376264 | tf_op jit(solution)/shard_map/ppermute | solution.py:28
  51.4 0.0 collective-permute-done.7
  51.4 2.3 %collective-permute-done.5 = f32[320,256]{1,0:T(8,128)} collective-permute-done((f32[320,256]{1,0:T(8,128)}, f32[320,256]{1,0:T(8,128)}, u32[]{:S(2)}, u32[]{:S(2)}) %collective-permute-start.5) | collective-permute-done | bytes 327712 | tf_op jit(solution)/shard_map/ppermute | solution.py:28
  53.7 1.0 add_add_fusion.1
  54.7 8.7 %collective-permute-done.3 = f32[448,256]{1,0:T(8,128)S(1)} collective-permute-done((f32[448,256]{1,0:T(8,128)S(1)}, f32[448,256]{1,0:T(8,128)S(1)}, u32[]{:S(2)}, u32[]{:S(2)}) %collective-permute-start.3) | collective-permute-done | bytes 458784 | tf_op jit(solution)/shard_map/ppermute | solution.py:28
  63.4 0.0 collective-permute-done.4
  63.4 0.1 add_add_fusion
  63.5 0.0 copy-start.1
  63.5 0.0 copy-start.2
  63.5 0.1 pad_maximum_fusion.1
  63.7 1.9 %collective-permute-start.8 = (f32[4,64,256]{2,1,0:T(8,128)S(1)}, f32[4,64,256]{2,1,0:T(8,128)S(1)}, u32[]{:S(2)}, u32[]{:S(2)}) collective-permute-start(f32[4,64,256]{2,1,0:T(8,128)S(1)} %get-tuple-element.53), channel_id=1, source_target_pairs={{0,16},{16,32},{32,48},{48,64},{64,80},{80,96},{96,112},{112,128},... | collective-permute-start | bytes 786440 | tf_op jit(solution)/shard_map/ppermute | solution.py:28
  65.6 5.3 %collective-permute-start.9 = (f32[4,64,256]{2,1,0:T(8,128)S(1)}, f32[4,64,256]{2,1,0:T(8,128)S(1)}, u32[]{:S(2)}, u32[]{:S(2)}) collective-permute-start(f32[4,64,256]{2,1,0:T(8,128)S(1)} %get-tuple-element.54), channel_id=1, source_target_pairs={{0,176},{16,0},{32,16},{48,32},{64,48},{80,64},{96,80},{112,96},{1... | collective-permute-start | bytes 786440 | tf_op jit(solution)/shard_map/ppermute | solution.py:28
  70.9 1.8 %collective-permute-done.8 = f32[4,64,256]{2,1,0:T(8,128)S(1)} collective-permute-done((f32[4,64,256]{2,1,0:T(8,128)S(1)}, f32[4,64,256]{2,1,0:T(8,128)S(1)}, u32[]{:S(2)}, u32[]{:S(2)}) %collective-permute-start.8) | collective-permute-done | bytes 262176 | tf_op jit(solution)/shard_map/ppermute | solution.py:28
  72.7 1.5 collective-permute-done.9
  74.2 0.1 fusion.2
  74.3 17.0 %all_to_all.30.pieces_ref = f32[4,64,256]{2,1,0:T(8,128)S(1)} all-to-all(f32[4,64,256]{2,1,0:T(8,128)S(1)} %fusion.2), channel_id=1, replica_groups={{0,48,96,144},{16,64,112,160},{32,80,128,176},{1,49,97,145},{17,65,113,..., dimensions={0} | all-to-all | bytes 524288 | tf_op jit(solution)/shard_map/all_to_all | solution.py:18
  91.3 0.0 copy-done.1
  91.3 0.0 copy-done.2
  91.3 0.3 shard_map.67
  91.6 14.6 %all_to_all.31.packed_ref = f32[8,32,128]{2,1,0:T(8,128)S(1)} all-to-all(f32[8,32,128]{2,1,0:T(8,128)S(1)} %get-tuple-element.35), channel_id=1, replica_groups=mesh['rep_x'=4,'rep_z'=12,'rep_core'=2,'shard'=8] {'shard'}, dimensions={0} | all-to-all | bytes 262144 | tf_op jit(solution)/shard_map/all_to_all | solution.py:18
  106.1 0.4 shard_map.68
  106.5 14.0 %all_to_all.32 = f32[8,8,384]{2,1,0:T(8,128)S(1)} all-to-all(f32[8,8,384]{2,1,0:T(8,128)S(1)} %bitcast.41), channel_id=1, replica_groups=mesh['rep_x'=4,'rep_z'=12,'rep_core'=2,'shard'=8] {'rep_x','rep_core'}, dimensions={0} | all-to-all | bytes 196608 | tf_op jit(solution)/shard_map/all_to_all | solution.py:18
  120.5 16.0 %all_to_all.33 = f32[12,8,384]{2,1,0:T(8,128)S(1)} all-to-all(f32[12,8,384]{2,1,0:T(8,128)S(1)} %broadcast_in_dim.4), channel_id=1, replica_groups=mesh['rep_x'=4,'rep_z'=12,'rep_core'=2,'shard'=8] {'rep_z'}, dimensions={0} | all-to-all | bytes 294912 | tf_op jit(solution)/shard_map/all_to_all | solution.py:18
  136.6 10.2 %all_to_all.34 = f32[8,8,384]{2,1,0:T(8,128)S(1)} all-to-all(f32[8,8,384]{2,1,0:T(8,128)S(1)} %broadcast_in_dim.5), channel_id=1, replica_groups=mesh['rep_x'=4,'rep_z'=12,'rep_core'=2,'shard'=8] {'rep_x','rep_core'}, dimensions={0} | all-to-all | bytes 196608 | tf_op jit(solution)/shard_map/all_to_all | solution.py:18
  146.7 5.2 %shard_map.69 = (f32[64,64]{1,0:T(8,128)S(1)}, f32[64,256]{1,0:T(8,128)S(1)}, f32[8,8,128]{2,1,0:T(8,128)S(1)}) custom-call(f32[64,384]{1,0:T(8,128)S(1)} %bitcast.40, f32[64,64]{1,0:T(8,128)S(1)} %get-tuple-element.38.left_ref), custom_call_target="tpu_custom_call" | custom-call | tf_op jit(solution)/shard_map/pallas_call | solution.py:219
  151.9 9.3 %all_to_all.35.squares_ref = f32[8,8,128]{2,1,0:T(8,128)S(1)} all-to-all(f32[8,8,128]{2,1,0:T(8,128)S(1)} %get-tuple-element.41), channel_id=1, replica_groups=mesh['rep_x'=4,'rep_z'=12,'rep_core'=2,'shard'=8] {'shard'}, dimensions={0} | all-to-all | bytes 65536 | tf_op jit(solution)/shard_map/all_to_all | solution.py:18
  161.2 0.9 shard_map.70
  (7 shorter events, 0.2 us)
Async XLA Ops:
  0.6 0.9 copy-start
  6.7 24.3 %collective-permute-start = (f32[3,768,256]{2,1,0:T(8,128)S(1)}, f32[3,768,256]{2,1,0:T(8,128)S(1)}, u32[]{:S(2)}, u32[]{:S(2)}) collective-permute-start(f32[3,768,256]{2,1,0:T(8,128)S(1)} %pad_maximum_fusion), channel_id=1, source_target_pairs={{0,8},{8,0},{1,9},{9,1},{2,10},{10,2},{3,11},{11,3},{4,12},{12,4},... | collective-permute-start | bytes 7077896 | tf_op jit(solution)/shard_map/ppermute | solution.py:28
  19.1 5.3 %collective-permute-start.1 = (f32[768,256]{1,0:T(8,128)S(1)}, f32[768,256]{1,0:T(8,128)S(1)}, u32[]{:S(2)}, u32[]{:S(2)}) collective-permute-start(f32[768,256]{1,0:T(8,128)S(1)} %bitcast.57), channel_id=1, source_target_pairs={{0,8},{8,0},{1,9},{9,1},{2,10},{10,2},{3,11},{11,3},{4,12},{12,4},... | collective-permute-start | bytes 2359304 | tf_op jit(solution)/shard_map/ppermute | solution.py:28
  24.4 14.8 %collective-permute-start.2 = (f32[448,256]{1,0:T(8,128)S(1)}, f32[448,256]{1,0:T(8,128)S(1)}, u32[]{:S(2)}, u32[]{:S(2)}) collective-permute-start(f32[448,256]{1,0:T(8,128)S(1)} %slice_add_fusion), channel_id=1, source_target_pairs={{0,192},{192,384},{384,576},{576,0},{1,193},{193,385},{385,577},{5... | collective-permute-start | bytes 1376264 | tf_op jit(solution)/shard_map/ppermute | solution.py:28
  26.4 13.0 %collective-permute-start.6 = (f32[320,256]{1,0:T(8,128)S(1)}, f32[320,256]{1,0:T(8,128)S(1)}, u32[]{:S(2)}, u32[]{:S(2)}) collective-permute-start(f32[320,256]{1,0:T(8,128)S(1)} %slice_add_fusion.1), channel_id=1, source_target_pairs={{0,576},{192,0},{384,192},{576,384},{1,577},{193,1},{385,193},{577... | collective-permute-start | bytes 983048 | tf_op jit(solution)/shard_map/ppermute | solution.py:28
  39.5 11.9 %collective-permute-start.7 = (f32[320,256]{1,0:T(8,128)S(1)}, f32[320,256]{1,0:T(8,128)S(1)}, u32[]{:S(2)}, u32[]{:S(2)}) collective-permute-start(f32[320,256]{1,0:T(8,128)S(1)} %fusion.1), channel_id=1, source_target_pairs={{0,576},{192,0},{384,192},{576,384},{1,577},{193,1},{385,193},{577... | collective-permute-start | bytes 983048 | tf_op jit(solution)/shard_map/ppermute | solution.py:28
  42.8 10.9 %collective-permute-start.5 = (f32[320,256]{1,0:T(8,128)}, f32[320,256]{1,0:T(8,128)}, u32[]{:S(2)}, u32[]{:S(2)}) collective-permute-start(f32[320,256]{1,0:T(8,128)} %bitcast_add_fusion.5), channel_id=1, source_target_pairs={{0,192},{192,384},{384,576},{576,0},{1,193},{193,385},{385,577},{5... | collective-permute-start | bytes 983048 | tf_op jit(solution)/shard_map/ppermute | solution.py:28
  44.8 18.6 %collective-permute-start.3 = (f32[448,256]{1,0:T(8,128)S(1)}, f32[448,256]{1,0:T(8,128)S(1)}, u32[]{:S(2)}, u32[]{:S(2)}) collective-permute-start(f32[448,256]{1,0:T(8,128)S(1)} %fusion), channel_id=1, source_target_pairs={{0,192},{192,384},{384,576},{576,0},{1,193},{193,385},{385,577},{5... | collective-permute-start | bytes 1376264 | tf_op jit(solution)/shard_map/ppermute | solution.py:28
  46.7 16.7 %collective-permute-start.4 = (f32[448,256]{1,0:T(8,128)S(1)}, f32[448,256]{1,0:T(8,128)S(1)}, u32[]{:S(2)}, u32[]{:S(2)}) collective-permute-start(f32[448,256]{1,0:T(8,128)S(1)} %bitcast_add_fusion.2), channel_id=1, source_target_pairs={{0,576},{192,0},{384,192},{576,384},{1,577},{193,1},{385,193},{577... | collective-permute-start | bytes 1376264 | tf_op jit(solution)/shard_map/ppermute | solution.py:28
  63.5 27.8 %copy-start.1 = (f32[64,256]{1,0:T(8,128)S(1)}, f32[64,256]{1,0:T(8,128)}, u32[]{:S(2)}) copy-start(f32[64,256]{1,0:T(8,128)} %momentum_ref.1) | copy-start | bytes 196612
  63.5 27.8 %copy-start.2 = (f32[256,64]{0,1:T(8,128)S(1)}, f32[256,64]{0,1:T(8,128)}, u32[]{:S(2)}) copy-start(f32[256,64]{0,1:T(8,128)} %param.7) | copy-start | bytes 196612
  63.7 9.1 %collective-permute-start.8 = (f32[4,64,256]{2,1,0:T(8,128)S(1)}, f32[4,64,256]{2,1,0:T(8,128)S(1)}, u32[]{:S(2)}, u32[]{:S(2)}) collective-permute-start(f32[4,64,256]{2,1,0:T(8,128)S(1)} %get-tuple-element.53), channel_id=1, source_target_pairs={{0,16},{16,32},{32,48},{48,64},{64,80},{80,96},{96,112},{112,128},... | collective-permute-start | bytes 786440 | tf_op jit(solution)/shard_map/ppermute | solution.py:28
  65.6 8.6 %collective-permute-start.9 = (f32[4,64,256]{2,1,0:T(8,128)S(1)}, f32[4,64,256]{2,1,0:T(8,128)S(1)}, u32[]{:S(2)}, u32[]{:S(2)}) collective-permute-start(f32[4,64,256]{2,1,0:T(8,128)S(1)} %get-tuple-element.54), channel_id=1, source_target_pairs={{0,176},{16,0},{32,16},{48,32},{64,48},{80,64},{96,80},{112,96},{1... | collective-permute-start | bytes 786440 | tf_op jit(solution)/shard_map/ppermute | solution.py:28

commit v5 on v4

--- a/solution.py
+++ b/solution.py
@@ -38,7 +38,7 @@
     cols = inputs.shape[1]
     rows = cotangent.shape[1] // (nx * nz * 2)
     x, z, core = lax.axis_index(X), lax.axis_index(Z), lax.axis_index(CORE)
-    half = na * nb * rows * 7 // 12 // 8 * 8
+    half = na * nb * rows * 13 // 24 // 8 * 8
 
     partial = lax.dot_general(
         cotangent, inputs, (((0,), (0,)), ((), ())), preferred_element_type=jnp.float32
@@ -111,24 +111,41 @@
     blocks = [scaled[b * tile : (b + 1) * tile, :] for b in range(rank // tile)]
     row_of = lax.broadcasted_iota(jnp.int32, (tile, wide), 0)
     full_tile = functools.partial(jnp.broadcast_to, shape=(tile, wide))
-    for k in range(0, rank, 2):
+    for k in range(0, rank, 4):
         b, r = divmod(k, tile)
-        first, second = full_tile(blocks[b][r : r + 1, :]), full_tile(blocks[b][r + 1 : r + 2, :])
-        a, c = full_tile(first[:, k : k + 1]), full_tile(first[:, k + 1 : k + 2])
-        d = full_tile(second[:, k + 1 : k + 2])
-        det = a * d - c * c
+        r0, r1, r2, r3 = (full_tile(blocks[b][r + i : r + i + 1, :]) for i in range(4))
+
+        def at(row, j, k=k):
+            return full_tile(row[:, k + j : k + j + 1])
+
+        e00, e01, e02, e03 = (at(r0, j) for j in range(4))
+        e11, e12, e13 = (at(r1, j) for j in range(1, 4))
+        e22, e23, e33 = at(r2, 2), at(r2, 3), at(r3, 3)
+        det = e00 * e11 - e01 * e01
         inv = 1.0 / det
-        to_first = (d * first - c * second) * inv
-        to_second = (a * second - c * first) * inv
+        s0, s1 = e11 * r0 - e01 * r1, e00 * r1 - e01 * r0
+        u02, u03 = (e11 * e02 - e01 * e12) * inv, (e11 * e03 - e01 * e13) * inv
+        u12, u13 = (e00 * e12 - e01 * e02) * inv, (e00 * e13 - e01 * e03) * inv
+        f22 = e22 - e02 * u02 - e12 * u12
+        f23 = e23 - e02 * u03 - e12 * u13
+        f33 = e33 - e03 * u03 - e13 * u13
+        t0, t1 = s0 * inv, s1 * inv
+        r2, r3 = r2 - e02 * t0 - e12 * t1, r3 - e03 * t0 - e13 * t1
+        second = f22 * f33 - f23 * f23
+        inv = 1.0 / second
+        s3 = f22 * r3 - f23 * r2
+        t2, t3 = (f33 * r2 - f23 * r3) * inv, s3 * inv
+        t0, t1 = t0 - u02 * t2 - u03 * t3, t1 - u12 * t2 - u13 * t3
         for i in range(b, rank // tile):
             old = blocks[i]
-            new = old - full_tile(old[:, k : k + 1]) * to_first
-            new = new - full_tile(old[:, k + 1 : k + 2]) * to_second
+            new = (old - at(old, 0) * t0 - at(old, 1) * t1) - (at(old, 2) * t2 + at(old, 3) * t3)
             if i == b:
-                root = lax.rsqrt(a)
-                new = jnp.where(row_of > r + 1, new, old)
-                new = jnp.where(row_of == r, first * root, new)
-                new = jnp.where(row_of == r + 1, (a * second - c * first) * (root * lax.rsqrt(det)), new)
+                root, later = lax.rsqrt(e00), lax.rsqrt(f22)
+                new = jnp.where(row_of > r + 3, new, old)
+                new = jnp.where(row_of == r, r0 * root, new)
+                new = jnp.where(row_of == r + 1, s1 * (root * lax.rsqrt(det)), new)
+                new = jnp.where(row_of == r + 2, r2 * later, new)
+                new = jnp.where(row_of == r + 3, s3 * (later * lax.rsqrt(second)), new)
             blocks[i] = new
     inverse = jnp.concatenate(blocks, axis=0)[:, rank:]
     ortho_ref[...] = lax.dot_general(

time: 163 us -> 162 us (level)
  Pallas kernels: 6.72 us -> 4.98 us
    pallas_call x1, Pallas kernels: 5.16 us -> 3.41 us  [body(): local_kernel(eliminate, f32((rows, rank)), f32((rank, cols)), f32((shards...]
where the time goes in v5:
time: 162 us
  blocking collectives  81 us (50%)
  starting transfers between devices  41.1 us (25%)
  waiting for transfers between devices  24.8 us (15%)
  Pallas kernels  4.98 us (3%)
  matrix products  4.17 us (3%)
  other arithmetic  2.67 us (2%)
  local copies, waits for them, and re-layouts  1.74 us (1%)
    all_to_all x6, blocking collectives, exchanged(): lax.all_to_all(pieces, axis, 0, 0, tiled=True, axis_index_groups=groups)  81 us
    ppermute x10, starting transfers between devices, sent(): lax.ppermute(value, axis, [(i, (i + distance) % size) for i in range(size)])  41.1 us
    ppermute x10, waiting for transfers between devices, sent(): lax.ppermute(value, axis, [(i, (i + distance) % size) for i in range(size)])  24.8 us
    dot_general x1, matrix products, gradient_rows(): lax.dot_general(cotangent, inputs, (((0,), (0,)), ((), ())), preferred_el...  4.17 us
    pallas_call x1, Pallas kernels, body(): local_kernel(eliminate, f32((rows, rank)), f32((rank, cols)), f32((shards...  3.41 us
  transfers between devices with their start and end apart: 10, of which 6 were waited for; matrix products, arithmetic and copies ran while one was open for 1% of the time, Pallas kernels for 0%

profile of v5, /device:TPU:1, one launch (start us, length us, event | category | flops | bytes accessed | tf_op | source)
XLA Modules:
  0.0 161.6 jit_solution(4880507164759557883)
XLA Ops:
  0.6 0.0 copy-start
  0.7 0.8 copy-done
  1.6 4.2 %fusion.3 = f32[6144,256]{1,0:T(8,128)S(1)} fusion(bf16[384,6144]{1,0:T(8,128)(2,1)} %param.5, bf16[384,256]{1,0:T(8,128)(2,1)S(1)} %copy-done), kind=kOutput, calls=%fused_computation.26 | convolution fusion | flops 1207959552 | bytes 11206656 | tf_op jit(solution)/shard_map/dot_general | solution.py:43
  5.7 0.8 constant_dynamic-slice_fusion
  6.6 0.2 pad_maximum_fusion
  6.7 12.4 %collective-permute-start = (f32[3,768,256]{2,1,0:T(8,128)S(1)}, f32[3,768,256]{2,1,0:T(8,128)S(1)}, u32[]{:S(2)}, u32[]{:S(2)}) collective-permute-start(f32[3,768,256]{2,1,0:T(8,128)S(1)} %pad_maximum_fusion), channel_id=1, source_target_pairs={{0,8},{8,0},{1,9},{9,1},{2,10},{10,2},{3,11},{11,3},{4,12},{12,4},... | collective-permute-start | bytes 7077896 | tf_op jit(solution)/shard_map/ppermute | solution.py:28
  19.1 1.9 %collective-permute-start.1 = (f32[768,256]{1,0:T(8,128)S(1)}, f32[768,256]{1,0:T(8,128)S(1)}, u32[]{:S(2)}, u32[]{:S(2)}) collective-permute-start(f32[768,256]{1,0:T(8,128)S(1)} %bitcast.57), channel_id=1, source_target_pairs={{0,8},{8,0},{1,9},{9,1},{2,10},{10,2},{3,11},{11,3},{4,12},{12,4},... | collective-permute-start | bytes 2359304 | tf_op jit(solution)/shard_map/ppermute | solution.py:28
  21.0 3.3 %collective-permute-done.1 = f32[768,256]{1,0:T(8,128)S(1)} collective-permute-done((f32[768,256]{1,0:T(8,128)S(1)}, f32[768,256]{1,0:T(8,128)S(1)}, u32[]{:S(2)}, u32[]{:S(2)}) %collective-permute-start.1) | collective-permute-done | bytes 786464 | tf_op jit(solution)/shard_map/ppermute | solution.py:28
  24.4 0.1 slice_add_fusion
  24.4 1.9 %collective-permute-start.2 = (f32[416,256]{1,0:T(8,128)S(1)}, f32[416,256]{1,0:T(8,128)S(1)}, u32[]{:S(2)}, u32[]{:S(2)}) collective-permute-start(f32[416,256]{1,0:T(8,128)S(1)} %slice_add_fusion), channel_id=1, source_target_pairs={{0,192},{192,384},{384,576},{576,0},{1,193},{193,385},{385,577},{5... | collective-permute-start | bytes 1277960 | tf_op jit(solution)/shard_map/ppermute | solution.py:28
  26.4 0.1 slice_add_fusion.1
  26.4 4.6 %collective-permute-start.6 = (f32[352,256]{1,0:T(8,128)S(1)}, f32[352,256]{1,0:T(8,128)S(1)}, u32[]{:S(2)}, u32[]{:S(2)}) collective-permute-start(f32[352,256]{1,0:T(8,128)S(1)} %slice_add_fusion.1), channel_id=1, source_target_pairs={{0,576},{192,0},{384,192},{576,384},{1,577},{193,1},{385,193},{577... | collective-permute-start | bytes 1081352 | tf_op jit(solution)/shard_map/ppermute | solution.py:28
  31.0 0.0 collective-permute-done
  31.0 0.1 bitcast_add_fusion.2
  31.1 0.1 bitcast_add_fusion.1
  31.2 7.4 %collective-permute-done.2 = f32[416,256]{1,0:T(8,128)S(1)} collective-permute-done((f32[416,256]{1,0:T(8,128)S(1)}, f32[416,256]{1,0:T(8,128)S(1)}, u32[]{:S(2)}, u32[]{:S(2)}) %collective-permute-start.2) | collective-permute-done | bytes 426016 | tf_op jit(solution)/shard_map/ppermute | solution.py:28
  38.5 0.1 fusion
  38.7 0.0 collective-permute-done.6
  38.7 0.8 fusion.1
  39.5 4.7 %collective-permute-start.7 = (f32[352,256]{1,0:T(8,128)}, f32[352,256]{1,0:T(8,128)S(1)}, u32[]{:S(2)}, u32[]{:S(2)}) collective-permute-start(f32[352,256]{1,0:T(8,128)} %fusion.1), channel_id=1, source_target_pairs={{0,576},{192,0},{384,192},{576,384},{1,577},{193,1},{385,193},{577... | collective-permute-start | bytes 1081352 | tf_op jit(solution)/shard_map/ppermute | solution.py:28
  44.2 1.9 %collective-permute-start.5 = (f32[352,256]{1,0:T(8,128)S(1)}, f32[352,256]{1,0:T(8,128)}, u32[]{:S(2)}, u32[]{:S(2)}) collective-permute-start(f32[352,256]{1,0:T(8,128)S(1)} %bitcast_add_fusion.5), channel_id=1, source_target_pairs={{0,192},{192,384},{384,576},{576,0},{1,193},{193,385},{385,577},{5... | collective-permute-start | bytes 1081352 | tf_op jit(solution)/shard_map/ppermute | solution.py:28
  46.2 1.9 %collective-permute-start.3 = (f32[416,256]{1,0:T(8,128)S(1)}, f32[416,256]{1,0:T(8,128)S(1)}, u32[]{:S(2)}, u32[]{:S(2)}) collective-permute-start(f32[416,256]{1,0:T(8,128)S(1)} %fusion), channel_id=1, source_target_pairs={{0,192},{192,384},{384,576},{576,0},{1,193},{193,385},{385,577},{5... | collective-permute-start | bytes 1277960 | tf_op jit(solution)/shard_map/ppermute | solution.py:28
  48.1 4.6 %collective-permute-start.4 = (f32[416,256]{1,0:T(8,128)S(1)}, f32[416,256]{1,0:T(8,128)S(1)}, u32[]{:S(2)}, u32[]{:S(2)}) collective-permute-start(f32[416,256]{1,0:T(8,128)S(1)} %bitcast_add_fusion.2), channel_id=1, source_target_pairs={{0,576},{192,0},{384,192},{576,384},{1,577},{193,1},{385,193},{577... | collective-permute-start | bytes 1277960 | tf_op jit(solution)/shard_map/ppermute | solution.py:28
  52.7 0.0 collective-permute-done.7
  52.7 2.9 %collective-permute-done.5 = f32[352,256]{1,0:T(8,128)} collective-permute-done((f32[352,256]{1,0:T(8,128)S(1)}, f32[352,256]{1,0:T(8,128)}, u32[]{:S(2)}, u32[]{:S(2)}) %collective-permute-start.5) | collective-permute-done | bytes 360480 | tf_op jit(solution)/shard_map/ppermute | solution.py:28
  55.6 1.1 add_add_fusion.1
  56.7 8.0 %collective-permute-done.3 = f32[416,256]{1,0:T(8,128)S(1)} collective-permute-done((f32[416,256]{1,0:T(8,128)S(1)}, f32[416,256]{1,0:T(8,128)S(1)}, u32[]{:S(2)}, u32[]{:S(2)}) %collective-permute-start.3) | collective-permute-done | bytes 426016 | tf_op jit(solution)/shard_map/ppermute | solution.py:28
  64.6 0.0 collective-permute-done.4
  64.6 0.1 add_add_fusion
  64.7 0.0 copy-start.1
  64.7 0.0 copy-start.2
  64.8 0.1 pad_maximum_fusion.1
  64.9 1.9 %collective-permute-start.8 = (f32[4,64,256]{2,1,0:T(8,128)S(1)}, f32[4,64,256]{2,1,0:T(8,128)S(1)}, u32[]{:S(2)}, u32[]{:S(2)}) collective-permute-start(f32[4,64,256]{2,1,0:T(8,128)S(1)} %get-tuple-element.53), channel_id=1, source_target_pairs={{0,16},{16,32},{32,48},{48,64},{64,80},{80,96},{96,112},{112,128},... | collective-permute-start | bytes 786440 | tf_op jit(solution)/shard_map/ppermute | solution.py:28
  66.8 5.3 %collective-permute-start.9 = (f32[4,64,256]{2,1,0:T(8,128)S(1)}, f32[4,64,256]{2,1,0:T(8,128)S(1)}, u32[]{:S(2)}, u32[]{:S(2)}) collective-permute-start(f32[4,64,256]{2,1,0:T(8,128)S(1)} %get-tuple-element.54), channel_id=1, source_target_pairs={{0,176},{16,0},{32,16},{48,32},{64,48},{80,64},{96,80},{112,96},{1... | collective-permute-start | bytes 786440 | tf_op jit(solution)/shard_map/ppermute | solution.py:28
  72.2 1.8 %collective-permute-done.8 = f32[4,64,256]{2,1,0:T(8,128)S(1)} collective-permute-done((f32[4,64,256]{2,1,0:T(8,128)S(1)}, f32[4,64,256]{2,1,0:T(8,128)S(1)}, u32[]{:S(2)}, u32[]{:S(2)}) %collective-permute-start.8) | collective-permute-done | bytes 262176 | tf_op jit(solution)/shard_map/ppermute | solution.py:28
  73.9 1.5 collective-permute-done.9
  75.4 0.1 fusion.2
  75.5 17.0 %all_to_all.30.pieces_ref = f32[4,64,256]{2,1,0:T(8,128)S(1)} all-to-all(f32[4,64,256]{2,1,0:T(8,128)S(1)} %fusion.2), channel_id=1, replica_groups={{0,48,96,144},{16,64,112,160},{32,80,128,176},{1,49,97,145},{17,65,113,..., dimensions={0} | all-to-all | bytes 524288 | tf_op jit(solution)/shard_map/all_to_all | solution.py:18
  92.5 0.0 copy-done.1
  92.5 0.0 copy-done.2
  92.5 0.3 shard_map.67
  92.8 14.6 %all_to_all.31.packed_ref = f32[8,32,128]{2,1,0:T(8,128)S(1)} all-to-all(f32[8,32,128]{2,1,0:T(8,128)S(1)} %get-tuple-element.35), channel_id=1, replica_groups=mesh['rep_x'=4,'rep_z'=12,'rep_core'=2,'shard'=8] {'shard'}, dimensions={0} | all-to-all | bytes 262144 | tf_op jit(solution)/shard_map/all_to_all | solution.py:18
  107.3 0.4 shard_map.68
  107.7 14.0 %all_to_all.32 = f32[8,8,384]{2,1,0:T(8,128)S(1)} all-to-all(f32[8,8,384]{2,1,0:T(8,128)S(1)} %bitcast.41), channel_id=1, replica_groups=mesh['rep_x'=4,'rep_z'=12,'rep_core'=2,'shard'=8] {'rep_x','rep_core'}, dimensions={0} | all-to-all | bytes 196608 | tf_op jit(solution)/shard_map/all_to_all | solution.py:18
  121.7 16.0 %all_to_all.33 = f32[12,8,384]{2,1,0:T(8,128)S(1)} all-to-all(f32[12,8,384]{2,1,0:T(8,128)S(1)} %broadcast_in_dim.4), channel_id=1, replica_groups=mesh['rep_x'=4,'rep_z'=12,'rep_core'=2,'shard'=8] {'rep_z'}, dimensions={0} | all-to-all | bytes 294912 | tf_op jit(solution)/shard_map/all_to_all | solution.py:18
  137.8 10.2 %all_to_all.34 = f32[8,8,384]{2,1,0:T(8,128)S(1)} all-to-all(f32[8,8,384]{2,1,0:T(8,128)S(1)} %broadcast_in_dim.5), channel_id=1, replica_groups=mesh['rep_x'=4,'rep_z'=12,'rep_core'=2,'shard'=8] {'rep_x','rep_core'}, dimensions={0} | all-to-all | bytes 196608 | tf_op jit(solution)/shard_map/all_to_all | solution.py:18
  147.9 3.4 %shard_map.69 = (f32[64,64]{1,0:T(8,128)S(1)}, f32[64,256]{1,0:T(8,128)S(1)}, f32[8,8,128]{2,1,0:T(8,128)S(1)}) custom-call(f32[64,384]{1,0:T(8,128)S(1)} %bitcast.40, f32[64,64]{1,0:T(8,128)S(1)} %get-tuple-element.38.left_ref), custom_call_target="tpu_custom_call" | custom-call | tf_op jit(solution)/shard_map/pallas_call | solution.py:236
  151.3 9.3 %all_to_all.35.squares_ref = f32[8,8,128]{2,1,0:T(8,128)S(1)} all-to-all(f32[8,8,128]{2,1,0:T(8,128)S(1)} %get-tuple-element.41), channel_id=1, replica_groups=mesh['rep_x'=4,'rep_z'=12,'rep_core'=2,'shard'=8] {'shard'}, dimensions={0} | all-to-all | bytes 65536 | tf_op jit(solution)/shard_map/all_to_all | solution.py:18
  160.6 0.9 shard_map.70
  (7 shorter events, 0.2 us)
Async XLA Ops:
  0.6 0.9 copy-start
  6.7 24.3 %collective-permute-start = (f32[3,768,256]{2,1,0:T(8,128)S(1)}, f32[3,768,256]{2,1,0:T(8,128)S(1)}, u32[]{:S(2)}, u32[]{:S(2)}) collective-permute-start(f32[3,768,256]{2,1,0:T(8,128)S(1)} %pad_maximum_fusion), channel_id=1, source_target_pairs={{0,8},{8,0},{1,9},{9,1},{2,10},{10,2},{3,11},{11,3},{4,12},{12,4},... | collective-permute-start | bytes 7077896 | tf_op jit(solution)/shard_map/ppermute | solution.py:28
  19.1 5.3 %collective-permute-start.1 = (f32[768,256]{1,0:T(8,128)S(1)}, f32[768,256]{1,0:T(8,128)S(1)}, u32[]{:S(2)}, u32[]{:S(2)}) collective-permute-start(f32[768,256]{1,0:T(8,128)S(1)} %bitcast.57), channel_id=1, source_target_pairs={{0,8},{8,0},{1,9},{9,1},{2,10},{10,2},{3,11},{11,3},{4,12},{12,4},... | collective-permute-start | bytes 2359304 | tf_op jit(solution)/shard_map/ppermute | solution.py:28
  24.4 14.1 %collective-permute-start.2 = (f32[416,256]{1,0:T(8,128)S(1)}, f32[416,256]{1,0:T(8,128)S(1)}, u32[]{:S(2)}, u32[]{:S(2)}) collective-permute-start(f32[416,256]{1,0:T(8,128)S(1)} %slice_add_fusion), channel_id=1, source_target_pairs={{0,192},{192,384},{384,576},{576,0},{1,193},{193,385},{385,577},{5... | collective-permute-start | bytes 1277960 | tf_op jit(solution)/shard_map/ppermute | solution.py:28
  26.4 12.3 %collective-permute-start.6 = (f32[352,256]{1,0:T(8,128)S(1)}, f32[352,256]{1,0:T(8,128)S(1)}, u32[]{:S(2)}, u32[]{:S(2)}) collective-permute-start(f32[352,256]{1,0:T(8,128)S(1)} %slice_add_fusion.1), channel_id=1, source_target_pairs={{0,576},{192,0},{384,192},{576,384},{1,577},{193,1},{385,193},{577... | collective-permute-start | bytes 1081352 | tf_op jit(solution)/shard_map/ppermute | solution.py:28
  39.5 13.2 %collective-permute-start.7 = (f32[352,256]{1,0:T(8,128)}, f32[352,256]{1,0:T(8,128)S(1)}, u32[]{:S(2)}, u32[]{:S(2)}) collective-permute-start(f32[352,256]{1,0:T(8,128)} %fusion.1), channel_id=1, source_target_pairs={{0,576},{192,0},{384,192},{576,384},{1,577},{193,1},{385,193},{577... | collective-permute-start | bytes 1081352 | tf_op jit(solution)/shard_map/ppermute | solution.py:28
  44.2 11.4 %collective-permute-start.5 = (f32[352,256]{1,0:T(8,128)S(1)}, f32[352,256]{1,0:T(8,128)}, u32[]{:S(2)}, u32[]{:S(2)}) collective-permute-start(f32[352,256]{1,0:T(8,128)S(1)} %bitcast_add_fusion.5), channel_id=1, source_target_pairs={{0,192},{192,384},{384,576},{576,0},{1,193},{193,385},{385,577},{5... | collective-permute-start | bytes 1081352 | tf_op jit(solution)/shard_map/ppermute | solution.py:28
  46.2 18.5 %collective-permute-start.3 = (f32[416,256]{1,0:T(8,128)S(1)}, f32[416,256]{1,0:T(8,128)S(1)}, u32[]{:S(2)}, u32[]{:S(2)}) collective-permute-start(f32[416,256]{1,0:T(8,128)S(1)} %fusion), channel_id=1, source_target_pairs={{0,192},{192,384},{384,576},{576,0},{1,193},{193,385},{385,577},{5... | collective-permute-start | bytes 1277960 | tf_op jit(solution)/shard_map/ppermute | solution.py:28
  48.1 16.6 %collective-permute-start.4 = (f32[416,256]{1,0:T(8,128)S(1)}, f32[416,256]{1,0:T(8,128)S(1)}, u32[]{:S(2)}, u32[]{:S(2)}) collective-permute-start(f32[416,256]{1,0:T(8,128)S(1)} %bitcast_add_fusion.2), channel_id=1, source_target_pairs={{0,576},{192,0},{384,192},{576,384},{1,577},{193,1},{385,193},{577... | collective-permute-start | bytes 1277960 | tf_op jit(solution)/shard_map/ppermute | solution.py:28
  64.7 27.8 %copy-start.1 = (f32[64,256]{1,0:T(8,128)S(1)}, f32[64,256]{1,0:T(8,128)}, u32[]{:S(2)}) copy-start(f32[64,256]{1,0:T(8,128)} %momentum_ref.1) | copy-start | bytes 196612
  64.7 27.8 %copy-start.2 = (f32[256,64]{0,1:T(8,128)S(1)}, f32[256,64]{0,1:T(8,128)}, u32[]{:S(2)}) copy-start(f32[256,64]{0,1:T(8,128)} %param.7) | copy-start | bytes 196612
  64.9 9.1 %collective-permute-start.8 = (f32[4,64,256]{2,1,0:T(8,128)S(1)}, f32[4,64,256]{2,1,0:T(8,128)S(1)}, u32[]{:S(2)}, u32[]{:S(2)}) collective-permute-start(f32[4,64,256]{2,1,0:T(8,128)S(1)} %get-tuple-element.53), channel_id=1, source_target_pairs={{0,16},{16,32},{32,48},{48,64},{64,80},{80,96},{96,112},{112,128},... | collective-permute-start | bytes 786440 | tf_op jit(solution)/shard_map/ppermute | solution.py:28
  66.8 8.6 %collective-permute-start.9 = (f32[4,64,256]{2,1,0:T(8,128)S(1)}, f32[4,64,256]{2,1,0:T(8,128)S(1)}, u32[]{:S(2)}, u32[]{:S(2)}) collective-permute-start(f32[4,64,256]{2,1,0:T(8,128)S(1)} %get-tuple-element.54), channel_id=1, source_target_pairs={{0,176},{16,0},{32,16},{48,32},{64,48},{80,64},{96,80},{112,96},{1... | collective-permute-start | bytes 786440 | tf_op jit(solution)/shard_map/ppermute | solution.py:28

commit v6 on v5

--- a/solution.py
+++ b/solution.py
@@ -38,7 +38,7 @@
     cols = inputs.shape[1]
     rows = cotangent.shape[1] // (nx * nz * 2)
     x, z, core = lax.axis_index(X), lax.axis_index(Z), lax.axis_index(CORE)
-    half = na * nb * rows * 13 // 24 // 8 * 8
+    half = na * nb * rows * 7 // 12 // 8 * 8
 
     partial = lax.dot_general(
         cotangent, inputs, (((0,), (0,)), ((), ())), preferred_element_type=jnp.float32
@@ -58,22 +58,19 @@
     relay_up = sent(far_up, X, 1)
     relay_down = sent(far_down, X, -1)
     near = gated(near, far_up, far_down)
+    before_low = mine_before[:half] + near[0, :half]
     before_high = mine_before[half:] + near[0, half:]
     after_low = mine_after[:half] + near[1, :half]
+    after_high = mine_after[half:] + near[1, half:]
     high_below = sent(before_high, X, 1)
     low_above = sent(after_low, X, -1)
-    near = gated(near, before_high, after_low)
-    own_low = lax.optimization_barrier(mine[:half] + near[2, :half])
-    near = gated(near, own_low)
-    before_low = lax.optimization_barrier(mine_before[:half] + near[0, :half] + relay_up)
-    low_below = sent(before_low, X, 1)
-    near = gated(near, before_low)
-    own_high = lax.optimization_barrier(mine[half:] + near[2, half:])
-    near = gated(near, own_high)
-    after_high = lax.optimization_barrier(mine_after[half:] + near[1, half:] + relay_down)
-    high_above = sent(after_high, X, -1)
-    low = own_low + low_below + low_above
-    high = own_high + high_below + high_above
+    relay_up = gated(relay_up, before_low, before_high, after_low)
+    low_below = sent(before_low + relay_up, X, 1)
+    relay_down = gated(relay_down, after_high, before_high, after_low)
+    high_above = sent(after_high + relay_down, X, -1)
+    own = lax.optimization_barrier(mine + near[2])
+    low = own[:half] + low_below + low_above
+    high = own[half:] + high_below + high_above
     over_x = jnp.concatenate([low, high], axis=0).reshape(na, nb, rows, cols)
 
     kind = z % nb

time: 162 us -> 163 us (level)
  waiting for transfers between devices: 24.8 us -> 20.7 us
  other arithmetic: 2.67 us -> 6.42 us
    ppermute x10, waiting for transfers between devices: 24.8 us -> 20.7 us  [sent(): lax.ppermute(value, axis, [(i, (i + distance) % size) for i in range(size)])]
    add x7 -> x6, other arithmetic: 2.22 us -> 4.37 us  [the longest x1 1.22 us: gradient_rows(): low_below = sent(before_low + relay_up, X, 1)]
  transfers between devices with their start and end apart: 10 -> 10, of which waited for: 6 -> 6; matrix products, arithmetic and copies ran while one was open for 1% -> 4% of each run, Pallas kernels for 0% -> 0%
where the time goes in v6:
time: 163 us; the launch traced here: 162 us
  blocking collectives  81.4 us (50%)
  starting transfers between devices  41.7 us (26%)
  waiting for transfers between devices  20.7 us (13%)
  other arithmetic  6.42 us (4%)
  Pallas kernels  4.98 us (3%)
  matrix products  4.17 us (3%)
  local copies, waits for them, and re-layouts  1.73 us (1%)
    all_to_all x6, blocking collectives, exchanged(): lax.all_to_all(pieces, axis, 0, 0, tiled=True, axis_index_groups=groups)  81.4 us
    ppermute x10, starting transfers between devices, sent(): lax.ppermute(value, axis, [(i, (i + distance) % size) for i in range(size)])  41.7 us
    ppermute x10, waiting for transfers between devices, sent(): lax.ppermute(value, axis, [(i, (i + distance) % size) for i in range(size)])  20.7 us
    dot_general x1, matrix products, gradient_rows(): lax.dot_general(cotangent, inputs, (((0,), (0,)), ((), ())), preferred_el...  4.17 us
    pallas_call x1, Pallas kernels, body(): local_kernel(eliminate, f32((rows, rank)), f32((rank, cols)), f32((shards...  3.41 us
  transfers between devices with their start and end apart: 10, of which 6 were waited for; matrix products, arithmetic and copies ran while one was open for 4% of the time, Pallas kernels for 0%

profile of v6, /device:TPU:1, one launch (start us, length us, event | category | flops | bytes accessed | tf_op | source)
XLA Modules:
  0.0 162.2 jit_solution(5255158584052606212)
XLA Ops:
  0.6 0.0 copy-start
  0.7 0.8 copy-done
  1.6 4.2 %fusion.3 = f32[6144,256]{1,0:T(8,128)S(1)} fusion(bf16[384,6144]{1,0:T(8,128)(2,1)} %param.5, bf16[384,256]{1,0:T(8,128)(2,1)S(1)} %copy-done), kind=kOutput, calls=%fused_computation.25 | convolution fusion | flops 1207959552 | bytes 11206656 | tf_op jit(solution)/shard_map/dot_general | solution.py:43
  5.7 0.8 constant_dynamic-slice_fusion
  6.6 0.2 pad_maximum_fusion
  6.7 12.4 %collective-permute-start = (f32[3,768,256]{2,1,0:T(8,128)S(1)}, f32[3,768,256]{2,1,0:T(8,128)S(1)}, u32[]{:S(2)}, u32[]{:S(2)}) collective-permute-start(f32[3,768,256]{2,1,0:T(8,128)S(1)} %pad_maximum_fusion), channel_id=1, source_target_pairs={{0,8},{8,0},{1,9},{9,1},{2,10},{10,2},{3,11},{11,3},{4,12},{12,4},... | collective-permute-start | bytes 7077896 | tf_op jit(solution)/shard_map/ppermute | solution.py:28
  19.1 1.9 %collective-permute-start.1 = (f32[768,256]{1,0:T(8,128)S(1)}, f32[768,256]{1,0:T(8,128)S(1)}, u32[]{:S(2)}, u32[]{:S(2)}) collective-permute-start(f32[768,256]{1,0:T(8,128)S(1)} %bitcast.50), channel_id=1, source_target_pairs={{0,8},{8,0},{1,9},{9,1},{2,10},{10,2},{3,11},{11,3},{4,12},{12,4},... | collective-permute-start | bytes 2359304 | tf_op jit(solution)/shard_map/ppermute | solution.py:28
  21.0 3.3 %collective-permute-done.1 = f32[768,256]{1,0:T(8,128)S(1)} collective-permute-done((f32[768,256]{1,0:T(8,128)S(1)}, f32[768,256]{1,0:T(8,128)S(1)}, u32[]{:S(2)}, u32[]{:S(2)}) %collective-permute-start.1) | collective-permute-done | bytes 786464 | tf_op jit(solution)/shard_map/ppermute | solution.py:28
  24.4 0.8 slice_add_fusion.1
  25.2 1.9 %collective-permute-start.2 = (f32[448,256]{1,0:T(8,128)}, f32[448,256]{1,0:T(8,128)}, u32[]{:S(2)}, u32[]{:S(2)}) collective-permute-start(f32[448,256]{1,0:T(8,128)} %slice_add_fusion.1), channel_id=1, source_target_pairs={{0,192},{192,384},{384,576},{576,0},{1,193},{193,385},{385,577},{5... | collective-permute-start | bytes 1376264 | tf_op jit(solution)/shard_map/ppermute | solution.py:28
  27.2 4.6 %collective-permute-start.6 = (f32[320,256]{1,0:T(8,128)S(1)}, f32[320,256]{1,0:T(8,128)S(1)}, u32[]{:S(2)}, u32[]{:S(2)}) collective-permute-start(f32[320,256]{1,0:T(8,128)S(1)} %slice_add_fusion.3), channel_id=1, source_target_pairs={{0,576},{192,0},{384,192},{576,384},{1,577},{193,1},{385,193},{577... | collective-permute-start | bytes 983048 | tf_op jit(solution)/shard_map/ppermute | solution.py:28
  31.7 0.0 collective-permute-done
  31.8 0.9 bitcast_add_fusion.4
  32.6 1.0 bitcast_add_fusion.2
  33.7 4.5 %collective-permute-done.6 = f32[320,256]{1,0:T(8,128)S(1)} collective-permute-done((f32[320,256]{1,0:T(8,128)S(1)}, f32[320,256]{1,0:T(8,128)S(1)}, u32[]{:S(2)}, u32[]{:S(2)}) %collective-permute-start.6) | collective-permute-done | bytes 327712 | tf_op jit(solution)/shard_map/ppermute | solution.py:28
  38.1 0.8 add.205
  38.9 5.3 %collective-permute-start.7 = (f32[320,256]{1,0:T(8,128)}, f32[320,256]{1,0:T(8,128)}, u32[]{:S(2)}, u32[]{:S(2)}) collective-permute-start(f32[320,256]{1,0:T(8,128)} %add.205), channel_id=1, source_target_pairs={{0,576},{192,0},{384,192},{576,384},{1,577},{193,1},{385,193},{577... | collective-permute-start | bytes 983048 | tf_op jit(solution)/shard_map/ppermute | solution.py:28
  44.2 1.9 %collective-permute-start.5 = (f32[320,256]{1,0:T(8,128)}, f32[320,256]{1,0:T(8,128)}, u32[]{:S(2)}, u32[]{:S(2)}) collective-permute-start(f32[320,256]{1,0:T(8,128)} %get-tuple-element.51), channel_id=1, source_target_pairs={{0,192},{192,384},{384,576},{576,0},{1,193},{193,385},{385,577},{5... | collective-permute-start | bytes 983048 | tf_op jit(solution)/shard_map/ppermute | solution.py:28
  46.2 4.6 %collective-permute-start.4 = (f32[448,256]{1,0:T(8,128)}, f32[448,256]{1,0:T(8,128)S(1)}, u32[]{:S(2)}, u32[]{:S(2)}) collective-permute-start(f32[448,256]{1,0:T(8,128)} %get-tuple-element.50), channel_id=1, source_target_pairs={{0,576},{192,0},{384,192},{576,384},{1,577},{193,1},{385,193},{577... | collective-permute-start | bytes 1376264 | tf_op jit(solution)/shard_map/ppermute | solution.py:28
  50.8 0.0 collective-permute-done.2
  50.8 1.2 add.200
  52.0 1.9 %collective-permute-start.3 = (f32[448,256]{1,0:T(8,128)S(1)}, f32[448,256]{1,0:T(8,128)S(1)}, u32[]{:S(2)}, u32[]{:S(2)}) collective-permute-start(f32[448,256]{1,0:T(8,128)S(1)} %add.200), channel_id=1, source_target_pairs={{0,192},{192,384},{384,576},{576,0},{1,193},{193,385},{385,577},{5... | collective-permute-start | bytes 1376264 | tf_op jit(solution)/shard_map/ppermute | solution.py:28
  54.0 0.1 bitcast_add_fusion
  54.1 0.0 collective-permute-done.7
  54.1 1.0 collective-permute-done.5
  55.1 1.1 fusion.1
  56.3 8.6 %collective-permute-done.3 = f32[448,256]{1,0:T(8,128)S(1)} collective-permute-done((f32[448,256]{1,0:T(8,128)S(1)}, f32[448,256]{1,0:T(8,128)S(1)}, u32[]{:S(2)}, u32[]{:S(2)}) %collective-permute-start.3) | collective-permute-done | bytes 458784 | tf_op jit(solution)/shard_map/ppermute | solution.py:28
  64.9 0.0 collective-permute-done.4
  64.9 0.1 fusion
  65.0 0.0 copy-start.1
  65.0 0.0 copy-start.2
  65.0 0.1 pad_maximum_fusion.1
  65.1 1.9 %collective-permute-start.8 = (f32[4,64,256]{2,1,0:T(8,128)S(1)}, f32[4,64,256]{2,1,0:T(8,128)S(1)}, u32[]{:S(2)}, u32[]{:S(2)}) collective-permute-start(f32[4,64,256]{2,1,0:T(8,128)S(1)} %get-tuple-element.53), channel_id=1, source_target_pairs={{0,16},{16,32},{32,48},{48,64},{64,80},{80,96},{96,112},{112,128},... | collective-permute-start | bytes 786440 | tf_op jit(solution)/shard_map/ppermute | solution.py:28
  67.0 5.3 %collective-permute-start.9 = (f32[4,64,256]{2,1,0:T(8,128)S(1)}, f32[4,64,256]{2,1,0:T(8,128)S(1)}, u32[]{:S(2)}, u32[]{:S(2)}) collective-permute-start(f32[4,64,256]{2,1,0:T(8,128)S(1)} %get-tuple-element.54), channel_id=1, source_target_pairs={{0,176},{16,0},{32,16},{48,32},{64,48},{80,64},{96,80},{112,96},{1... | collective-permute-start | bytes 786440 | tf_op jit(solution)/shard_map/ppermute | solution.py:28
  72.4 1.8 %collective-permute-done.8 = f32[4,64,256]{2,1,0:T(8,128)S(1)} collective-permute-done((f32[4,64,256]{2,1,0:T(8,128)S(1)}, f32[4,64,256]{2,1,0:T(8,128)S(1)}, u32[]{:S(2)}, u32[]{:S(2)}) %collective-permute-start.8) | collective-permute-done | bytes 262176 | tf_op jit(solution)/shard_map/ppermute | solution.py:28
  74.2 1.5 collective-permute-done.9
  75.7 0.1 fusion.2
  75.7 16.9 %all_to_all.30.pieces_ref = f32[4,64,256]{2,1,0:T(8,128)S(1)} all-to-all(f32[4,64,256]{2,1,0:T(8,128)S(1)} %fusion.2), channel_id=1, replica_groups={{0,48,96,144},{16,64,112,160},{32,80,128,176},{1,49,97,145},{17,65,113,..., dimensions={0} | all-to-all | bytes 524288 | tf_op jit(solution)/shard_map/all_to_all | solution.py:18
  92.6 0.0 copy-done.1
  92.6 0.0 copy-done.2
  92.6 0.3 shard_map.67
  92.9 14.6 %all_to_all.31.packed_ref = f32[8,32,128]{2,1,0:T(8,128)S(1)} all-to-all(f32[8,32,128]{2,1,0:T(8,128)S(1)} %get-tuple-element.31), channel_id=1, replica_groups=mesh['rep_x'=4,'rep_z'=12,'rep_core'=2,'shard'=8] {'shard'}, dimensions={0} | all-to-all | bytes 262144 | tf_op jit(solution)/shard_map/all_to_all | solution.py:18
  107.5 0.4 shard_map.68
  107.8 14.1 %all_to_all.32 = f32[8,8,384]{2,1,0:T(8,128)S(1)} all-to-all(f32[8,8,384]{2,1,0:T(8,128)S(1)} %bitcast.35), channel_id=1, replica_groups=mesh['rep_x'=4,'rep_z'=12,'rep_core'=2,'shard'=8] {'rep_x','rep_core'}, dimensions={0} | all-to-all | bytes 196608 | tf_op jit(solution)/shard_map/all_to_all | solution.py:18
  122.0 16.4 %all_to_all.33 = f32[12,8,384]{2,1,0:T(8,128)S(1)} all-to-all(f32[12,8,384]{2,1,0:T(8,128)S(1)} %broadcast_in_dim.4), channel_id=1, replica_groups=mesh['rep_x'=4,'rep_z'=12,'rep_core'=2,'shard'=8] {'rep_z'}, dimensions={0} | all-to-all | bytes 294912 | tf_op jit(solution)/shard_map/all_to_all | solution.py:18
  138.4 10.2 %all_to_all.34 = f32[8,8,384]{2,1,0:T(8,128)S(1)} all-to-all(f32[8,8,384]{2,1,0:T(8,128)S(1)} %broadcast_in_dim.5), channel_id=1, replica_groups=mesh['rep_x'=4,'rep_z'=12,'rep_core'=2,'shard'=8] {'rep_x','rep_core'}, dimensions={0} | all-to-all | bytes 196608 | tf_op jit(solution)/shard_map/all_to_all | solution.py:18
  148.6 3.4 %shard_map.69 = (f32[64,64]{1,0:T(8,128)S(1)}, f32[64,256]{1,0:T(8,128)S(1)}, f32[8,8,128]{2,1,0:T(8,128)S(1)}) custom-call(f32[64,384]{1,0:T(8,128)S(1)} %bitcast.34, f32[64,64]{1,0:T(8,128)S(1)} %get-tuple-element.34.left_ref), custom_call_target="tpu_custom_call" | custom-call | tf_op jit(solution)/shard_map/pallas_call | solution.py:233
  152.0 9.3 %all_to_all.35.squares_ref = f32[8,8,128]{2,1,0:T(8,128)S(1)} all-to-all(f32[8,8,128]{2,1,0:T(8,128)S(1)} %get-tuple-element.37), channel_id=1, replica_groups=mesh['rep_x'=4,'rep_z'=12,'rep_core'=2,'shard'=8] {'shard'}, dimensions={0} | all-to-all | bytes 65536 | tf_op jit(solution)/shard_map/all_to_all | solution.py:18
  161.3 0.9 shard_map.70
  (6 shorter events, 0.1 us)
Async XLA Ops:
  0.6 0.9 copy-start
  6.7 25.0 %collective-permute-start = (f32[3,768,256]{2,1,0:T(8,128)S(1)}, f32[3,768,256]{2,1,0:T(8,128)S(1)}, u32[]{:S(2)}, u32[]{:S(2)}) collective-permute-start(f32[3,768,256]{2,1,0:T(8,128)S(1)} %pad_maximum_fusion), channel_id=1, source_target_pairs={{0,8},{8,0},{1,9},{9,1},{2,10},{10,2},{3,11},{11,3},{4,12},{12,4},... | collective-permute-start | bytes 7077896 | tf_op jit(solution)/shard_map/ppermute | solution.py:28
  19.1 5.3 %collective-permute-start.1 = (f32[768,256]{1,0:T(8,128)S(1)}, f32[768,256]{1,0:T(8,128)S(1)}, u32[]{:S(2)}, u32[]{:S(2)}) collective-permute-start(f32[768,256]{1,0:T(8,128)S(1)} %bitcast.50), channel_id=1, source_target_pairs={{0,8},{8,0},{1,9},{9,1},{2,10},{10,2},{3,11},{11,3},{4,12},{12,4},... | collective-permute-start | bytes 2359304 | tf_op jit(solution)/shard_map/ppermute | solution.py:28
  25.2 25.6 %collective-permute-start.2 = (f32[448,256]{1,0:T(8,128)}, f32[448,256]{1,0:T(8,128)}, u32[]{:S(2)}, u32[]{:S(2)}) collective-permute-start(f32[448,256]{1,0:T(8,128)} %slice_add_fusion.1), channel_id=1, source_target_pairs={{0,192},{192,384},{384,576},{576,0},{1,193},{193,385},{385,577},{5... | collective-permute-start | bytes 1376264 | tf_op jit(solution)/shard_map/ppermute | solution.py:28
  27.2 11.0 %collective-permute-start.6 = (f32[320,256]{1,0:T(8,128)S(1)}, f32[320,256]{1,0:T(8,128)S(1)}, u32[]{:S(2)}, u32[]{:S(2)}) collective-permute-start(f32[320,256]{1,0:T(8,128)S(1)} %slice_add_fusion.3), channel_id=1, source_target_pairs={{0,576},{192,0},{384,192},{576,384},{1,577},{193,1},{385,193},{577... | collective-permute-start | bytes 983048 | tf_op jit(solution)/shard_map/ppermute | solution.py:28
  38.9 15.2 %collective-permute-start.7 = (f32[320,256]{1,0:T(8,128)}, f32[320,256]{1,0:T(8,128)}, u32[]{:S(2)}, u32[]{:S(2)}) collective-permute-start(f32[320,256]{1,0:T(8,128)} %add.205), channel_id=1, source_target_pairs={{0,576},{192,0},{384,192},{576,384},{1,577},{193,1},{385,193},{577... | collective-permute-start | bytes 983048 | tf_op jit(solution)/shard_map/ppermute | solution.py:28
  44.2 10.9 %collective-permute-start.5 = (f32[320,256]{1,0:T(8,128)}, f32[320,256]{1,0:T(8,128)}, u32[]{:S(2)}, u32[]{:S(2)}) collective-permute-start(f32[320,256]{1,0:T(8,128)} %get-tuple-element.51), channel_id=1, source_target_pairs={{0,192},{192,384},{384,576},{576,0},{1,193},{193,385},{385,577},{5... | collective-permute-start | bytes 983048 | tf_op jit(solution)/shard_map/ppermute | solution.py:28
  46.2 18.6 %collective-permute-start.4 = (f32[448,256]{1,0:T(8,128)}, f32[448,256]{1,0:T(8,128)S(1)}, u32[]{:S(2)}, u32[]{:S(2)}) collective-permute-start(f32[448,256]{1,0:T(8,128)} %get-tuple-element.50), channel_id=1, source_target_pairs={{0,576},{192,0},{384,192},{576,384},{1,577},{193,1},{385,193},{577... | collective-permute-start | bytes 1376264 | tf_op jit(solution)/shard_map/ppermute | solution.py:28
  52.0 12.8 %collective-permute-start.3 = (f32[448,256]{1,0:T(8,128)S(1)}, f32[448,256]{1,0:T(8,128)S(1)}, u32[]{:S(2)}, u32[]{:S(2)}) collective-permute-start(f32[448,256]{1,0:T(8,128)S(1)} %add.200), channel_id=1, source_target_pairs={{0,192},{192,384},{384,576},{576,0},{1,193},{193,385},{385,577},{5... | collective-permute-start | bytes 1376264 | tf_op jit(solution)/shard_map/ppermute | solution.py:28
  65.0 27.7 %copy-start.1 = (f32[64,256]{1,0:T(8,128)S(1)}, f32[64,256]{1,0:T(8,128)}, u32[]{:S(2)}) copy-start(f32[64,256]{1,0:T(8,128)} %momentum_ref.1) | copy-start | bytes 196612
  65.0 27.7 %copy-start.2 = (f32[256,64]{0,1:T(8,128)S(1)}, f32[256,64]{0,1:T(8,128)}, u32[]{:S(2)}) copy-start(f32[256,64]{0,1:T(8,128)} %param.7) | copy-start | bytes 196612
  65.1 9.1 %collective-permute-start.8 = (f32[4,64,256]{2,1,0:T(8,128)S(1)}, f32[4,64,256]{2,1,0:T(8,128)S(1)}, u32[]{:S(2)}, u32[]{:S(2)}) collective-permute-start(f32[4,64,256]{2,1,0:T(8,128)S(1)} %get-tuple-element.53), channel_id=1, source_target_pairs={{0,16},{16,32},{32,48},{48,64},{64,80},{80,96},{96,112},{112,128},... | collective-permute-start | bytes 786440 | tf_op jit(solution)/shard_map/ppermute | solution.py:28
  67.0 8.6 %collective-permute-start.9 = (f32[4,64,256]{2,1,0:T(8,128)S(1)}, f32[4,64,256]{2,1,0:T(8,128)S(1)}, u32[]{:S(2)}, u32[]{:S(2)}) collective-permute-start(f32[4,64,256]{2,1,0:T(8,128)S(1)} %get-tuple-element.54), channel_id=1, source_target_pairs={{0,176},{16,0},{32,16},{48,32},{64,48},{80,64},{96,80},{112,96},{1... | collective-permute-start | bytes 786440 | tf_op jit(solution)/shard_map/ppermute | solution.py:28

commit v7 on v6

--- a/solution.py
+++ b/solution.py
@@ -44,20 +44,20 @@
         cotangent, inputs, (((0,), (0,)), ((), ())), preferred_element_type=jnp.float32
     ).reshape(nx, na, nb, 2, rows, cols)
 
-    def piece(ahead, which):
-        at_x = lax.dynamic_index_in_dim(partial, (x + ahead) % nx, 0, keepdims=False)
+    def piece(ahead, which, source=partial):
+        at_x = lax.dynamic_index_in_dim(source, (x + ahead) % nx, 0, keepdims=False)
         return lax.dynamic_index_in_dim(at_x, which, 2, keepdims=False).reshape(-1, cols)
 
     near = jnp.stack([piece(ahead, 1 - core) for ahead in (1, 3, 0)])
-    far, near, mine_far, mine_before, mine_after, mine = lax.optimization_barrier(
-        (piece(2, 1 - core), near, *(piece(ahead, core) for ahead in (2, 1, 3, 0)))
-    )
+    far, near, mine_far = lax.optimization_barrier((piece(2, 1 - core), near, piece(2, core)))
     far = sent(far, CORE, 1)
     near = sent(near, CORE, 1)
     far_up, far_down = mine_far[:half] + far[:half], mine_far[half:] + far[half:]
     relay_up = sent(far_up, X, 1)
     relay_down = sent(far_down, X, -1)
     near = gated(near, far_up, far_down)
+    later = gated(partial, far_up, far_down)
+    mine_before, mine_after, mine = (piece(ahead, core, later) for ahead in (1, 3, 0))
     before_low = mine_before[:half] + near[0, :half]
     before_high = mine_before[half:] + near[0, half:]
     after_low = mine_after[:half] + near[1, :half]

time: 163 us -> 159 us (0.975)
  blocking collectives: 81.4 us -> 77.3 us
  waiting for transfers between devices: 20.7 us -> 22.6 us
    all_to_all x6, blocking collectives: 81.4 us -> 77.3 us  [exchanged(): lax.all_to_all(pieces, axis, 0, 0, tiled=True, axis_index_groups=groups)]
    ppermute x10, waiting for transfers between devices: 20.7 us -> 22.6 us  [sent(): lax.ppermute(value, axis, [(i, (i + distance) % size) for i in range(size)])]
  transfers between devices with their start and end apart: 10 -> 10, of which waited for: 6 -> 7; matrix products, arithmetic and copies ran while one was open for 4% -> 4% of each run, Pallas kernels for 0% -> 0%
where the time goes in v7:
time: 159 us
  blocking collectives  77.3 us (49%)
  starting transfers between devices  40.4 us (25%)
  waiting for transfers between devices  22.6 us (14%)
  other arithmetic  6.37 us (4%)
  Pallas kernels  4.97 us (3%)
  matrix products  4.17 us (3%)
  local copies, waits for them, and re-layouts  1.6 us (1%)
    all_to_all x6, blocking collectives, exchanged(): lax.all_to_all(pieces, axis, 0, 0, tiled=True, axis_index_groups=groups)  77.3 us
    ppermute x10, starting transfers between devices, sent(): lax.ppermute(value, axis, [(i, (i + distance) % size) for i in range(size)])  40.4 us
    ppermute x10, waiting for transfers between devices, sent(): lax.ppermute(value, axis, [(i, (i + distance) % size) for i in range(size)])  22.6 us
    dot_general x1, matrix products, gradient_rows(): lax.dot_general(cotangent, inputs, (((0,), (0,)), ((), ())), preferred_el...  4.17 us
    pallas_call x1, Pallas kernels, body(): local_kernel(eliminate, f32((rows, rank)), f32((rank, cols)), f32((shards...  3.41 us
  transfers between devices with their start and end apart: 10, of which 7 were waited for; matrix products, arithmetic and copies ran while one was open for 4% of the time, Pallas kernels for 0%

profile of v7, /device:TPU:1, one launch (start us, length us, event | category | flops | bytes accessed | tf_op | source)
XLA Modules:
  0.0 158.5 jit_solution(10541464895985488547)
XLA Ops:
  0.6 0.0 copy-start
  0.7 0.8 copy-done
  1.6 4.2 %fusion.3 = f32[6144,256]{1,0:T(8,128)S(1)} fusion(bf16[384,6144]{1,0:T(8,128)(2,1)} %param.5, bf16[384,256]{1,0:T(8,128)(2,1)S(1)} %copy-done), kind=kOutput, calls=%fused_computation.25 | convolution fusion | flops 1207959552 | bytes 11206656 | tf_op jit(solution)/shard_map/dot_general | solution.py:43
  5.7 0.5 constant_dynamic-slice_fusion.3
  6.2 0.2 pad_maximum_fusion
  6.4 12.4 %collective-permute-start.1 = (f32[3,768,256]{2,1,0:T(8,128)S(1)}, f32[3,768,256]{2,1,0:T(8,128)S(1)}, u32[]{:S(2)}, u32[]{:S(2)}) collective-permute-start(f32[3,768,256]{2,1,0:T(8,128)S(1)} %pad_maximum_fusion), channel_id=1, source_target_pairs={{0,8},{8,0},{1,9},{9,1},{2,10},{10,2},{3,11},{11,3},{4,12},{12,4},... | collective-permute-start | bytes 7077896 | tf_op jit(solution)/shard_map/ppermute | solution.py:28
  18.8 1.9 %collective-permute-start = (f32[768,256]{1,0:T(8,128)S(1)}, f32[768,256]{1,0:T(8,128)S(1)}, u32[]{:S(2)}, u32[]{:S(2)}) collective-permute-start(f32[768,256]{1,0:T(8,128)S(1)} %bitcast.51), channel_id=1, source_target_pairs={{0,8},{8,0},{1,9},{9,1},{2,10},{10,2},{3,11},{11,3},{4,12},{12,4},... | collective-permute-start | bytes 2359304 | tf_op jit(solution)/shard_map/ppermute | solution.py:28
  20.7 3.3 %collective-permute-done = f32[768,256]{1,0:T(8,128)S(1)} collective-permute-done((f32[768,256]{1,0:T(8,128)S(1)}, f32[768,256]{1,0:T(8,128)S(1)}, u32[]{:S(2)}, u32[]{:S(2)}) %collective-permute-start) | collective-permute-done | bytes 786464 | tf_op jit(solution)/shard_map/ppermute | solution.py:28
  24.1 1.9 %collective-permute-start.6 = (f32[320,256]{1,0:T(8,128)S(1)}, f32[320,256]{1,0:T(8,128)S(1)}, u32[]{:S(2)}, u32[]{:S(2)}) collective-permute-start(f32[320,256]{1,0:T(8,128)S(1)} %slice_add_fusion.7), channel_id=1, source_target_pairs={{0,576},{192,0},{384,192},{576,384},{1,577},{193,1},{385,193},{577... | collective-permute-start | bytes 983048 | tf_op jit(solution)/shard_map/ppermute | solution.py:28
  26.0 0.8 slice_add_fusion.3
  26.8 3.4 %collective-permute-start.2 = (f32[448,256]{1,0:T(8,128)}, f32[448,256]{1,0:T(8,128)}, u32[]{:S(2)}, u32[]{:S(2)}) collective-permute-start(f32[448,256]{1,0:T(8,128)} %slice_add_fusion.3), channel_id=1, source_target_pairs={{0,192},{192,384},{384,576},{576,0},{1,193},{193,385},{385,577},{5... | collective-permute-start | bytes 1376264 | tf_op jit(solution)/shard_map/ppermute | solution.py:28
  30.2 0.2 constant_dynamic-slice_fusion.2
  30.4 0.0 collective-permute-done.1
  30.4 0.8 slice_add_fusion.6
  31.3 1.0 slice_add_fusion.1
  32.3 2.7 %collective-permute-done.6 = f32[320,256]{1,0:T(8,128)S(1)} collective-permute-done((f32[320,256]{1,0:T(8,128)S(1)}, f32[320,256]{1,0:T(8,128)S(1)}, u32[]{:S(2)}, u32[]{:S(2)}) %collective-permute-start.6) | collective-permute-done | bytes 327712 | tf_op jit(solution)/shard_map/ppermute | solution.py:28
  35.0 0.8 add.205
  35.8 3.3 %collective-permute-start.7 = (f32[320,256]{1,0:T(8,128)}, f32[320,256]{1,0:T(8,128)}, u32[]{:S(2)}, u32[]{:S(2)}) collective-permute-start(f32[320,256]{1,0:T(8,128)} %add.205), channel_id=1, source_target_pairs={{0,576},{192,0},{384,192},{576,384},{1,577},{193,1},{385,193},{577... | collective-permute-start | bytes 983048 | tf_op jit(solution)/shard_map/ppermute | solution.py:28
  39.1 2.0 %collective-permute-start.5 = (f32[320,256]{1,0:T(8,128)}, f32[320,256]{1,0:T(8,128)}, u32[]{:S(2)}, u32[]{:S(2)}) collective-permute-start(f32[320,256]{1,0:T(8,128)} %get-tuple-element.47), channel_id=1, source_target_pairs={{0,192},{192,384},{384,576},{576,0},{1,193},{193,385},{385,577},{5... | collective-permute-start | bytes 983048 | tf_op jit(solution)/shard_map/ppermute | solution.py:28
  41.1 4.5 %collective-permute-start.4 = (f32[448,256]{1,0:T(8,128)}, f32[448,256]{1,0:T(8,128)S(1)}, u32[]{:S(2)}, u32[]{:S(2)}) collective-permute-start(f32[448,256]{1,0:T(8,128)} %get-tuple-element.46), channel_id=1, source_target_pairs={{0,576},{192,0},{384,192},{576,384},{1,577},{193,1},{385,193},{577... | collective-permute-start | bytes 1376264 | tf_op jit(solution)/shard_map/ppermute | solution.py:28
  45.6 0.0 collective-permute-done.2
  45.7 1.2 add.200
  46.9 1.9 %collective-permute-start.3 = (f32[448,256]{1,0:T(8,128)S(1)}, f32[448,256]{1,0:T(8,128)S(1)}, u32[]{:S(2)}, u32[]{:S(2)}) collective-permute-start(f32[448,256]{1,0:T(8,128)S(1)} %add.200), channel_id=1, source_target_pairs={{0,192},{192,384},{384,576},{576,0},{1,193},{193,385},{385,577},{5... | collective-permute-start | bytes 1376264 | tf_op jit(solution)/shard_map/ppermute | solution.py:28
  48.8 0.1 bitcast_add_fusion
  48.9 0.0 collective-permute-done.7
  48.9 1.6 %collective-permute-done.5 = f32[320,256]{1,0:T(8,128)} collective-permute-done((f32[320,256]{1,0:T(8,128)}, f32[320,256]{1,0:T(8,128)}, u32[]{:S(2)}, u32[]{:S(2)}) %collective-permute-start.5) | collective-permute-done | bytes 327712 | tf_op jit(solution)/shard_map/ppermute | solution.py:28
  50.5 1.1 fusion.1
  51.7 4.2 %collective-permute-done.4 = f32[448,256]{1,0:T(8,128)S(1)} collective-permute-done((f32[448,256]{1,0:T(8,128)}, f32[448,256]{1,0:T(8,128)S(1)}, u32[]{:S(2)}, u32[]{:S(2)}) %collective-permute-start.4) | collective-permute-done | bytes 458784 | tf_op jit(solution)/shard_map/ppermute | solution.py:28
  55.8 4.4 %collective-permute-done.3 = f32[448,256]{1,0:T(8,128)S(1)} collective-permute-done((f32[448,256]{1,0:T(8,128)S(1)}, f32[448,256]{1,0:T(8,128)S(1)}, u32[]{:S(2)}, u32[]{:S(2)}) %collective-permute-start.3) | collective-permute-done | bytes 458784 | tf_op jit(solution)/shard_map/ppermute | solution.py:28
  60.3 0.1 fusion
  60.4 0.0 copy-start.1
  60.4 0.0 copy-start.2
  60.4 0.1 pad_maximum_fusion.1
  60.5 7.2 %collective-permute-start.9 = (f32[4,64,256]{2,1,0:T(8,128)S(1)}, f32[4,64,256]{2,1,0:T(8,128)S(1)}, u32[]{:S(2)}, u32[]{:S(2)}) collective-permute-start(f32[4,64,256]{2,1,0:T(8,128)S(1)} %get-tuple-element.50), channel_id=1, source_target_pairs={{0,176},{16,0},{32,16},{48,32},{64,48},{80,64},{96,80},{112,96},{1... | collective-permute-start | bytes 786440 | tf_op jit(solution)/shard_map/ppermute | solution.py:28
  67.7 1.9 %collective-permute-start.8 = (f32[4,64,256]{2,1,0:T(8,128)S(1)}, f32[4,64,256]{2,1,0:T(8,128)S(1)}, u32[]{:S(2)}, u32[]{:S(2)}) collective-permute-start(f32[4,64,256]{2,1,0:T(8,128)S(1)} %get-tuple-element.49), channel_id=1, source_target_pairs={{0,16},{16,32},{32,48},{48,64},{64,80},{80,96},{96,112},{112,128},... | collective-permute-start | bytes 786440 | tf_op jit(solution)/shard_map/ppermute | solution.py:28
  69.7 1.3 collective-permute-done.9
  71.0 5.0 %collective-permute-done.8 = f32[4,64,256]{2,1,0:T(8,128)S(1)} collective-permute-done((f32[4,64,256]{2,1,0:T(8,128)S(1)}, f32[4,64,256]{2,1,0:T(8,128)S(1)}, u32[]{:S(2)}, u32[]{:S(2)}) %collective-permute-start.8) | collective-permute-done | bytes 262176 | tf_op jit(solution)/shard_map/ppermute | solution.py:28
  76.1 0.1 fusion.2
  76.1 14.3 %all_to_all.30.pieces_ref = f32[4,64,256]{2,1,0:T(8,128)S(1)} all-to-all(f32[4,64,256]{2,1,0:T(8,128)S(1)} %fusion.2), channel_id=1, replica_groups={{0,48,96,144},{16,64,112,160},{32,80,128,176},{1,49,97,145},{17,65,113,..., dimensions={0} | all-to-all | bytes 524288 | tf_op jit(solution)/shard_map/all_to_all | solution.py:18
  90.4 0.0 copy-done.1
  90.4 0.0 copy-done.2
  90.5 0.3 shard_map.67
  90.7 14.6 %all_to_all.31.packed_ref = f32[8,32,128]{2,1,0:T(8,128)S(1)} all-to-all(f32[8,32,128]{2,1,0:T(8,128)S(1)} %get-tuple-element.27), channel_id=1, replica_groups=mesh['rep_x'=4,'rep_z'=12,'rep_core'=2,'shard'=8] {'shard'}, dimensions={0} | all-to-all | bytes 262144 | tf_op jit(solution)/shard_map/all_to_all | solution.py:18
  105.3 0.4 shard_map.68
  105.6 14.0 %all_to_all.32 = f32[8,8,384]{2,1,0:T(8,128)S(1)} all-to-all(f32[8,8,384]{2,1,0:T(8,128)S(1)} %bitcast.36), channel_id=1, replica_groups=mesh['rep_x'=4,'rep_z'=12,'rep_core'=2,'shard'=8] {'rep_x','rep_core'}, dimensions={0} | all-to-all | bytes 196608 | tf_op jit(solution)/shard_map/all_to_all | solution.py:18
  119.7 14.9 %all_to_all.33 = f32[12,8,384]{2,1,0:T(8,128)S(1)} all-to-all(f32[12,8,384]{2,1,0:T(8,128)S(1)} %broadcast_in_dim.4), channel_id=1, replica_groups=mesh['rep_x'=4,'rep_z'=12,'rep_core'=2,'shard'=8] {'rep_z'}, dimensions={0} | all-to-all | bytes 294912 | tf_op jit(solution)/shard_map/all_to_all | solution.py:18
  134.7 10.2 %all_to_all.34 = f32[8,8,384]{2,1,0:T(8,128)S(1)} all-to-all(f32[8,8,384]{2,1,0:T(8,128)S(1)} %broadcast_in_dim.5), channel_id=1, replica_groups=mesh['rep_x'=4,'rep_z'=12,'rep_core'=2,'shard'=8] {'rep_x','rep_core'}, dimensions={0} | all-to-all | bytes 196608 | tf_op jit(solution)/shard_map/all_to_all | solution.py:18
  144.8 3.4 %shard_map.69 = (f32[64,64]{1,0:T(8,128)S(1)}, f32[64,256]{1,0:T(8,128)S(1)}, f32[8,8,128]{2,1,0:T(8,128)S(1)}) custom-call(f32[64,384]{1,0:T(8,128)S(1)} %bitcast.35, f32[64,64]{1,0:T(8,128)S(1)} %get-tuple-element.30.left_ref), custom_call_target="tpu_custom_call" | custom-call | tf_op jit(solution)/shard_map/pallas_call | solution.py:233
  148.3 9.3 %all_to_all.35.squares_ref = f32[8,8,128]{2,1,0:T(8,128)S(1)} all-to-all(f32[8,8,128]{2,1,0:T(8,128)S(1)} %get-tuple-element.33), channel_id=1, replica_groups=mesh['rep_x'=4,'rep_z'=12,'rep_core'=2,'shard'=8] {'shard'}, dimensions={0} | all-to-all | bytes 65536 | tf_op jit(solution)/shard_map/all_to_all | solution.py:18
  157.6 0.9 shard_map.70
  (6 shorter events, 0.1 us)
Async XLA Ops:
  0.6 0.9 copy-start
  6.4 24.0 %collective-permute-start.1 = (f32[3,768,256]{2,1,0:T(8,128)S(1)}, f32[3,768,256]{2,1,0:T(8,128)S(1)}, u32[]{:S(2)}, u32[]{:S(2)}) collective-permute-start(f32[3,768,256]{2,1,0:T(8,128)S(1)} %pad_maximum_fusion), channel_id=1, source_target_pairs={{0,8},{8,0},{1,9},{9,1},{2,10},{10,2},{3,11},{11,3},{4,12},{12,4},... | collective-permute-start | bytes 7077896 | tf_op jit(solution)/shard_map/ppermute | solution.py:28
  18.8 5.3 %collective-permute-start = (f32[768,256]{1,0:T(8,128)S(1)}, f32[768,256]{1,0:T(8,128)S(1)}, u32[]{:S(2)}, u32[]{:S(2)}) collective-permute-start(f32[768,256]{1,0:T(8,128)S(1)} %bitcast.51), channel_id=1, source_target_pairs={{0,8},{8,0},{1,9},{9,1},{2,10},{10,2},{3,11},{11,3},{4,12},{12,4},... | collective-permute-start | bytes 2359304 | tf_op jit(solution)/shard_map/ppermute | solution.py:28
  24.1 10.9 %collective-permute-start.6 = (f32[320,256]{1,0:T(8,128)S(1)}, f32[320,256]{1,0:T(8,128)S(1)}, u32[]{:S(2)}, u32[]{:S(2)}) collective-permute-start(f32[320,256]{1,0:T(8,128)S(1)} %slice_add_fusion.7), channel_id=1, source_target_pairs={{0,576},{192,0},{384,192},{576,384},{1,577},{193,1},{385,193},{577... | collective-permute-start | bytes 983048 | tf_op jit(solution)/shard_map/ppermute | solution.py:28
  26.8 18.8 %collective-permute-start.2 = (f32[448,256]{1,0:T(8,128)}, f32[448,256]{1,0:T(8,128)}, u32[]{:S(2)}, u32[]{:S(2)}) collective-permute-start(f32[448,256]{1,0:T(8,128)} %slice_add_fusion.3), channel_id=1, source_target_pairs={{0,192},{192,384},{384,576},{576,0},{1,193},{193,385},{385,577},{5... | collective-permute-start | bytes 1376264 | tf_op jit(solution)/shard_map/ppermute | solution.py:28
  35.8 13.1 %collective-permute-start.7 = (f32[320,256]{1,0:T(8,128)}, f32[320,256]{1,0:T(8,128)}, u32[]{:S(2)}, u32[]{:S(2)}) collective-permute-start(f32[320,256]{1,0:T(8,128)} %add.205), channel_id=1, source_target_pairs={{0,576},{192,0},{384,192},{576,384},{1,577},{193,1},{385,193},{577... | collective-permute-start | bytes 983048 | tf_op jit(solution)/shard_map/ppermute | solution.py:28
  39.1 11.5 %collective-permute-start.5 = (f32[320,256]{1,0:T(8,128)}, f32[320,256]{1,0:T(8,128)}, u32[]{:S(2)}, u32[]{:S(2)}) collective-permute-start(f32[320,256]{1,0:T(8,128)} %get-tuple-element.47), channel_id=1, source_target_pairs={{0,192},{192,384},{384,576},{576,0},{1,193},{193,385},{385,577},{5... | collective-permute-start | bytes 983048 | tf_op jit(solution)/shard_map/ppermute | solution.py:28
  41.1 14.7 %collective-permute-start.4 = (f32[448,256]{1,0:T(8,128)}, f32[448,256]{1,0:T(8,128)S(1)}, u32[]{:S(2)}, u32[]{:S(2)}) collective-permute-start(f32[448,256]{1,0:T(8,128)} %get-tuple-element.46), channel_id=1, source_target_pairs={{0,576},{192,0},{384,192},{576,384},{1,577},{193,1},{385,193},{577... | collective-permute-start | bytes 1376264 | tf_op jit(solution)/shard_map/ppermute | solution.py:28
  46.9 13.4 %collective-permute-start.3 = (f32[448,256]{1,0:T(8,128)S(1)}, f32[448,256]{1,0:T(8,128)S(1)}, u32[]{:S(2)}, u32[]{:S(2)}) collective-permute-start(f32[448,256]{1,0:T(8,128)S(1)} %add.200), channel_id=1, source_target_pairs={{0,192},{192,384},{384,576},{576,0},{1,193},{193,385},{385,577},{5... | collective-permute-start | bytes 1376264 | tf_op jit(solution)/shard_map/ppermute | solution.py:28
  60.4 30.1 %copy-start.1 = (f32[64,256]{1,0:T(8,128)S(1)}, f32[64,256]{1,0:T(8,128)}, u32[]{:S(2)}) copy-start(f32[64,256]{1,0:T(8,128)} %momentum_ref.1) | copy-start | bytes 196612
  60.4 30.1 %copy-start.2 = (f32[256,64]{0,1:T(8,128)S(1)}, f32[256,64]{0,1:T(8,128)}, u32[]{:S(2)}) copy-start(f32[256,64]{0,1:T(8,128)} %param.7) | copy-start | bytes 196612
  60.5 10.5 %collective-permute-start.9 = (f32[4,64,256]{2,1,0:T(8,128)S(1)}, f32[4,64,256]{2,1,0:T(8,128)S(1)}, u32[]{:S(2)}, u32[]{:S(2)}) collective-permute-start(f32[4,64,256]{2,1,0:T(8,128)S(1)} %get-tuple-element.50), channel_id=1, source_target_pairs={{0,176},{16,0},{32,16},{48,32},{64,48},{80,64},{96,80},{112,96},{1... | collective-permute-start | bytes 786440 | tf_op jit(solution)/shard_map/ppermute | solution.py:28
  67.7 8.3 %collective-permute-start.8 = (f32[4,64,256]{2,1,0:T(8,128)S(1)}, f32[4,64,256]{2,1,0:T(8,128)S(1)}, u32[]{:S(2)}, u32[]{:S(2)}) collective-permute-start(f32[4,64,256]{2,1,0:T(8,128)S(1)} %get-tuple-element.49), channel_id=1, source_target_pairs={{0,16},{16,32},{32,48},{48,64},{64,80},{80,96},{96,112},{112,128},... | collective-permute-start | bytes 786440 | tf_op jit(solution)/shard_map/ppermute | solution.py:28
